TPU v7x, 512 devices: a 4x2x32 block of a 4x16x32 slice. The times are simulated.
512 devices in a mesh: grp: 2 (over y), pen: 128 (over x, z), ch: 2 (over core).
Axes of the slice: x: 4, y: 2, z: 32, core: 2. Of those that a mesh axis runs over, the one named last changes fastest.
The devices are a block of a 4x16x32 slice.
Arguments:
- features: bfloat16 [256, 32, 128, 256], P(('grp', 'pen'), 'ch'), parts along dimension 0, may hold values from -6 to 6
- spectral_weights: bfloat16 [1, 2, 16, 32, 32, 1024], P(None, None, None, None, 'ch', 'pen'), may hold values from -0.75 to 0.75
- bypass_weights: float32 [1, 32, 32], P(None, None, 'ch'), may hold values from -0.75 to 0.75
- bypass_bias: float32 [1, 32], P(None, 'ch'), may hold values from -1 to 1
Outputs:
- features_out: float32 [256, 32, 128, 256], P(('grp', 'pen'), 'ch'), parts along dimension 0
There are 2 independent parts, one for each index of `grp`. A program takes and returns all parts, laid end to end along the dimension named above; an argument that names none is the same for every part. Nothing has to cross between parts.
All inputs are finite; a program needn't handle non-finite values.
Results may differ from a plain program's by a relative error of at most 0.0003.
Values may be sent and summed in bfloat16 or wider, within the bound.
No kernel may reach another device: no remote copies, remote signals or barrier semaphores. Data moves between devices by JAX's collectives and lax.ppermute only.
A program may use at most 64 MiB of HBM per device.

v0:
```python
import math

import jax
import jax.numpy as jnp
from jax import lax
from jax.sharding import PartitionSpec as P

C = 32
NX = 128
NY = 128
NZ = 256
MX = 16
MY = 32
MZ = 32


HIGHEST = lax.Precision.HIGHEST


def sent_together(arrays, axis, split_dim, concat_dim, along):
    ends, at = ([], 0)
    for a in arrays[:-1]:
        at += a.shape[along]
        ends.append(at)
    both = jnp.concatenate(arrays, axis=along)
    return tuple(
        jnp.split(
            lax.all_to_all(both, axis, split_axis=split_dim, concat_axis=concat_dim, tiled=True),
            ends,
            axis=along,
        )
    )


def side_by_side(arrays, axis, dim, along):
    both = jnp.concatenate(arrays, axis=along)
    out, at, finished = (lax.all_gather(both, axis, axis=dim, tiled=True), 0, [])
    for a in arrays:
        finished.append(lax.slice_in_dim(out, at, at + a.shape[along], axis=along))
        at += a.shape[along]
    return tuple(finished)


def joined_along(blocks, dim):
    blocks = jnp.moveaxis(blocks, 0, dim)
    lengths = blocks.shape
    return blocks.reshape(*lengths[:dim], lengths[dim] * lengths[dim + 1], *lengths[dim + 2 :])


def copy_for_each(value, axis):
    size = lax.axis_size(axis)
    return lax.all_to_all(
        jnp.broadcast_to(value[None], (size, *value.shape)), axis, 0, 0, tiled=True
    )


def collect(value, axis, dim):
    return joined_along(copy_for_each(value, axis), dim)


def kept_freqs(length, kept_count):
    offsets = jnp.arange(kept_count, dtype=jnp.int32)
    return jnp.where(offsets < kept_count // 2, offsets, length - kept_count + offsets)


def tables(length, kept_count):
    phases = (
        kept_freqs(length, kept_count)[:, None]
        * jnp.arange(length, dtype=jnp.int32)[None, :]
        % length
    )
    angles = phases.astype(jnp.float32) * (2.0 * math.pi / length)
    return (jnp.cos(angles), jnp.sin(angles))


def z_forward(slabs, forward_z):
    outer, rows_count = (slabs.shape[0], slabs.shape[1])
    joined = jnp.dot(slabs.reshape(-1, NZ), forward_z, precision=HIGHEST)
    joined = joined.reshape(outer, rows_count, 2 * MZ)
    return (joined[:, :, :MZ], joined[:, :, MZ:])


def y_forward(real_z, imag_z, cos_y, sin_y):
    scale = NY ** (-0.5)
    real_y = (
        jnp.einsum("ay,pyk->pak", cos_y, real_z, precision=HIGHEST)
        + jnp.einsum("ay,pyk->pak", sin_y, imag_z, precision=HIGHEST)
    ) * scale
    imag_y = (
        jnp.einsum("ay,pyk->pak", cos_y, imag_z, precision=HIGHEST)
        - jnp.einsum("ay,pyk->pak", sin_y, real_z, precision=HIGHEST)
    ) * scale
    return (real_y.reshape(real_y.shape[0], MY * MZ), imag_y.reshape(imag_y.shape[0], MY * MZ))


def y_inverse(real_b, imag_b, cos_y, sin_y):
    scale = MY ** (-0.5)
    real_a = (
        jnp.einsum("ay,pak->pyk", cos_y, real_b, precision=HIGHEST)
        - jnp.einsum("ay,pak->pyk", sin_y, imag_b, precision=HIGHEST)
    ) * scale
    imag_a = (
        jnp.einsum("ay,pak->pyk", cos_y, imag_b, precision=HIGHEST)
        + jnp.einsum("ay,pak->pyk", sin_y, real_b, precision=HIGHEST)
    ) * scale
    return (real_a, imag_a)


def z_inverse(real_a, imag_a, inverse_z):
    outer, rows_count = (real_a.shape[0], real_a.shape[1])
    joined = jnp.concatenate([real_a, imag_a], axis=-1).reshape(-1, 2 * MZ)
    return jnp.dot(joined, inverse_z, precision=HIGHEST).reshape(outer, rows_count, NZ)


def mode_core(real_s, imag_s, weights, cos_x, sin_x):
    real_s, imag_s = sent_together((real_s, imag_s), "pen", 2, 0, 1)
    scale = NX ** (-0.5)
    real_x = (
        jnp.einsum("jx,xcq->jcq", cos_x, real_s, precision=HIGHEST)
        + jnp.einsum("jx,xcq->jcq", sin_x, imag_s, precision=HIGHEST)
    ) * scale
    imag_x = (
        jnp.einsum("jx,xcq->jcq", cos_x, imag_s, precision=HIGHEST)
        - jnp.einsum("jx,xcq->jcq", sin_x, real_s, precision=HIGHEST)
    ) * scale
    real_x, imag_x = side_by_side((real_x, imag_x), "ch", 1, 0)
    weight_re = weights[0].astype(jnp.float32)
    weight_im = weights[1].astype(jnp.float32)
    real_g = jnp.einsum("jiq,jioq->joq", real_x, weight_re, precision=HIGHEST) - jnp.einsum(
        "jiq,jioq->joq", imag_x, weight_im, precision=HIGHEST
    )
    imag_g = jnp.einsum("jiq,jioq->joq", imag_x, weight_re, precision=HIGHEST) + jnp.einsum(
        "jiq,jioq->joq", real_x, weight_im, precision=HIGHEST
    )
    scale_back = MX ** (-0.5)
    real_h = (
        jnp.einsum("jx,joq->xoq", cos_x, real_g, precision=HIGHEST)
        - jnp.einsum("jx,joq->xoq", sin_x, imag_g, precision=HIGHEST)
    ) * scale_back
    imag_h = (
        jnp.einsum("jx,joq->xoq", cos_x, imag_g, precision=HIGHEST)
        + jnp.einsum("jx,joq->xoq", sin_x, real_g, precision=HIGHEST)
    ) * scale_back
    return sent_together((real_h, imag_h), "pen", 0, 2, 1)


def local(features, spectral_weights, bypass_weights, bypass_bias):
    cos_x, sin_x = tables(NX, MX)
    cos_y, sin_y = tables(NY, MY)
    cos_z, sin_z = tables(NZ, MZ)
    forward_z = jnp.concatenate([cos_z.T, -sin_z.T], axis=1) * NZ ** (-0.5)
    inverse_z = jnp.concatenate([cos_z, -sin_z], axis=0) * MZ ** (-0.5)
    slabs = features.shape[0]
    local_ch = features.shape[1]
    current = features.astype(jnp.float32)
    real_z, imag_z = z_forward(current.reshape(slabs * local_ch, NY, NZ), forward_z)
    real_s, imag_s = y_forward(real_z, imag_z, cos_y, sin_y)
    real_b, imag_b = mode_core(
        real_s.reshape(slabs, local_ch, MY * MZ),
        imag_s.reshape(slabs, local_ch, MY * MZ),
        spectral_weights[0],
        cos_x,
        sin_x,
    )
    real_a, imag_a = y_inverse(
        real_b.reshape(slabs * local_ch, MY, MZ),
        imag_b.reshape(slabs * local_ch, MY, MZ),
        cos_y,
        sin_y,
    )
    spectral = z_inverse(real_a, imag_a, inverse_z).reshape(slabs, local_ch, NY, NZ)
    gathered = collect(current.astype(jnp.bfloat16), "ch", 1).astype(current.dtype)
    mixing = bypass_weights[0]
    bypass = jnp.einsum(
        "io,xin->xon", mixing, gathered.reshape(slabs, C, NY * NZ), precision=HIGHEST
    )
    offsets = bypass_bias[0][None, :, None, None]
    current = current + jax.nn.gelu(
        bypass.reshape(slabs, local_ch, NY, NZ) + offsets + spectral, approximate=True
    )
    return current


def solution(mesh):
    return jax.shard_map(
        local,
        mesh=mesh,
        in_specs=(
            P(("grp", "pen"), "ch", None, None),
            P(None, None, None, None, "ch", "pen"),
            P(None, None, "ch"),
            P(None, "ch"),
        ),
        out_specs=P(("grp", "pen"), "ch", None, None),
        check_vma=False,
    )
```

profile of v0, /device:TPU:40, one launch (start us, length us, event | category | flops | bytes accessed | tf_op | source)
XLA Modules:
  0.0 166.3 jit_solution(2380845330790645075)
XLA Ops:
  0.2 2.3 %convolution_bitcast_fusion = f32[8,8,16,128]{3,1,2,0:T(8,128)S(1)} fusion(bf16[2048,256]{1,0:T(8,128)(2,1)} %bitcast.133, f32[256,32]{0,1:T(8,128)S(1)} %get-tuple-element.20, f32[256,32]{0,1:T(8,128)S(1)} %get-tuple-element.19), kind=kOutput, calls=%fused_computation.16 | convolution fusion | flops 402685952 | bytes 1638400 | tf_op jit(solution)/shard_map/dot_general | solution.py:78
  2.7 0.5 fusion.29
  3.2 0.5 fusion.33
  5.6 0.5 broadcast.184
  6.2 2.0 %reduce.8 = f32[1024,32]{1,0:T(8,128)S(1)} reduce(f32[1024,1,32]{2,1,0:T(1,128)S(1)} %bitcast.138, f32[]{:T(128)} %broadcast.184), dimensions={1}, to_apply=%bitcast.118.reduce_sub_computation | reduce | bytes 262148
  8.1 0.9 reshape.87
  9.0 53.2 %all-to-all-start.1 = ((f32[128,1,256]{2,1,0:T(1,128)}), f32[128,1,256]{2,1,0:T(1,128)S(1)}, u32[]{:S(2)}, u32[]{:S(2)}) async-start(f32[128,1,256]{2,1,0:T(1,128)} %reshape.87), calls=%async_computation.1 | async-start | bytes 262144 | tf_op jit(solution)/shard_map/all_to_all | solution.py:28
  62.2 30.3 %all-to-all-done.1 = f32[128,1,256]{2,1,0:T(1,128)S(1)} async-done(((f32[128,1,256]{2,1,0:T(1,128)}), f32[128,1,256]{2,1,0:T(1,128)S(1)}, u32[]{:S(2)}, u32[]{:S(2)}) %all-to-all-start.1) | async-done | bytes 131104 | tf_op jit(solution)/shard_map/all_to_all | solution.py:28
  92.6 1.6 broadcast_in_dim.5
  94.2 3.8 %all-to-all-start = ((bf16[2,1,16,128,256]{4,3,2,1,0:T(8,128)(2,1)}), bf16[2,1,16,128,256]{4,3,2,1,0:T(8,128)(2,1)S(1)}, u32[]{:S(2)}, u32[]{:S(2)}) async-start(bf16[2,1,16,128,256]{4,3,2,1,0:T(8,128)(2,1)} %broadcast_in_dim.5), calls=%async_computation | async-start | bytes 4194304 | tf_op jit(solution)/shard_map/all_to_all | solution.py:52
  98.0 0.9 reduce.9
  98.9 1.7 %reshape.88 = f32[1024,1,32]{2,1,0:T(1,128)} reshape(f32[128,256]{1,0:T(8,128)S(1)} %reduce.9) | data formatting | bytes 262144
  100.6 1.2 copy.39
  103.2 2.3 %all_gather.3 = f32[32,32,8]{0,1,2:T(8,128)S(1)} all-gather(f32[32,16,8]{0,1,2:T(8,128)S(1)} %pad_maximum_fusion.2), channel_id=1, replica_groups=mesh['grp'=2,'pen'=128,'ch'=2] {'ch'}, dimensions={1}, use_global_device_ids=true | all-gather | bytes 49152 | tf_op jit(solution)/shard_map/all_gather | solution.py:37
  105.6 0.7 copy.96
  106.3 0.7 copy.95
  107.0 3.1 %fusion.24 = (f32[16,8,16]{1,2,0:T(8,128)S(1)}, f32[16,8,16]{1,2,0:T(8,128)}, f32[16,8,16]{1,2,0:T(8,128)S(1)}, f32[16,8,16]{1,2,0:T(8,128)}) fusion(f32[16,8,32]{2,1,0:T(8,128)} %copy.96, bf16[1,2,16,32,16,8]{3,5,4,2,1,0:T(8,128)(2,1)} %param.5, f32[16,8,32]{2,1,0:T(8,128)} %copy.95), kind=kLoop, calls=%fused_computation.39 | loop fusion | flops 647168 | bytes 327680
  110.1 1.0 copy.70
  111.2 1.0 copy.54
  113.7 1.0 copy.40
  114.7 1.9 %reshape.89 = f32[128,1,256]{2,1,0:T(1,128)} reshape(f32[128,8,32]{2,1,0:T(8,128)} %bitcast.136) | data formatting | bytes 262144
  116.7 10.1 %all-to-all-start.2 = ((f32[128,1,256]{2,1,0:T(1,128)}), f32[128,1,256]{2,1,0:T(1,128)S(1)}, u32[]{:S(2)}, u32[]{:S(2)}) async-start(f32[128,1,256]{2,1,0:T(1,128)} %reshape.89), calls=%async_computation.2 | async-start | bytes 262144 | tf_op jit(solution)/shard_map/all_to_all | solution.py:28
  126.8 1.2 copy.99
  128.0 1.0 fusion.100
  129.0 1.9 %copy.100 = f32[2,8,128,256]{3,2,1,0:T(8,128)} copy(f32[2,8,128,256]{3,1,2,0:T(8,128)S(1)} %bitcast.132) | data formatting | bytes 4194304
  131.2 26.5 %all-to-all-done.2 = f32[128,1,256]{2,1,0:T(1,128)S(1)} async-done(((f32[128,1,256]{2,1,0:T(1,128)}), f32[128,1,256]{2,1,0:T(1,128)S(1)}, u32[]{:S(2)}, u32[]{:S(2)}) %all-to-all-start.2) | async-done | bytes 131104 | tf_op jit(solution)/shard_map/all_to_all | solution.py:28
  157.7 0.9 reduce.10
  159.3 0.6 fusion.78
  160.2 0.6 fusion.80
  160.9 0.6 fusion.11
  161.5 0.6 fusion.13
  162.2 4.1 %fusion.8 = f32[1,16,128,256]{3,2,1,0:T(8,128)} fusion(f32[2,8,128,256]{3,2,1,0:T(8,128)S(1)} %copy-done.2, bf16[1,16,128,256]{3,2,1,0:T(8,128)(2,1)S(1)} %copy-done.1, f32[16]{0:T(128)S(1)} %bitcast.145, f32[16,128,32]{1,2,0:T(8,128)S(1)} %fusion.11, f32[16,128,32]{1,2,0:T(8,128)S(1)} %fusion.13, f32[32,256]{1,0:T(8,128)S(1)} %get-tuple-element.18, ...), kind=kOutput, calls=%fused_computation.9 | convolution fusion | flops 409108480 | bytes 5832768 | tf_op jit(solution)/shard_map/dot_general | solution.py:112
  (46 shorter events, 6.4 us)
Async XLA Ops:
  0.0 128.0 %copy-start = (f32[1,32,16]{1,2,0:T(8,128)S(1)}, f32[1,32,16]{1,2,0:T(8,128)}, u32[]{:S(2)}) copy-start(f32[1,32,16]{1,2,0:T(8,128)} %param.6) | copy-start | bytes 6148
  0.0 2.6 %copy-start.3 = (s32[32]{0:T(128)}, s32[32]{0:T(128)S(1)}, u32[]{:S(2)}) copy-start(s32[32]{0:T(128)S(1)} %compare_select_fusion.2) | copy-start | bytes 388
  4.5 88.1 %copy-start.1 = (bf16[1,16,128,256]{3,2,1,0:T(8,128)(2,1)S(1)}, bf16[1,16,128,256]{3,2,1,0:T(8,128)(2,1)}, u32[]{:S(2)}) copy-start(bf16[1,16,128,256]{3,2,1,0:T(8,128)(2,1)} %param.4) | copy-start | bytes 3145732
  9.0 83.5 %all-to-all-start.1 = ((f32[128,1,256]{2,1,0:T(1,128)}), f32[128,1,256]{2,1,0:T(1,128)S(1)}, u32[]{:S(2)}, u32[]{:S(2)}) async-start(f32[128,1,256]{2,1,0:T(1,128)} %reshape.87), calls=%async_computation.1 | async-start | bytes 262144 | tf_op jit(solution)/shard_map/all_to_all | solution.py:28
  94.2 22.5 %all-to-all-start = ((bf16[2,1,16,128,256]{4,3,2,1,0:T(8,128)(2,1)}), bf16[2,1,16,128,256]{4,3,2,1,0:T(8,128)(2,1)S(1)}, u32[]{:S(2)}, u32[]{:S(2)}) async-start(bf16[2,1,16,128,256]{4,3,2,1,0:T(8,128)(2,1)} %broadcast_in_dim.5), calls=%async_computation | async-start | bytes 4194304 | tf_op jit(solution)/shard_map/all_to_all | solution.py:52
  116.7 41.0 %all-to-all-start.2 = ((f32[128,1,256]{2,1,0:T(1,128)}), f32[128,1,256]{2,1,0:T(1,128)S(1)}, u32[]{:S(2)}, u32[]{:S(2)}) async-start(f32[128,1,256]{2,1,0:T(1,128)} %reshape.89), calls=%async_computation.2 | async-start | bytes 262144 | tf_op jit(solution)/shard_map/all_to_all | solution.py:28
  129.0 2.0 %copy-start.4 = (s32[32]{0:T(128)S(1)}, s32[32]{0:T(128)}, u32[]{:S(2)}) copy-start(s32[32]{0:T(128)} %copy-done.3) | copy-start | bytes 388
  159.0 3.1 %copy-start.5 = (f32[1,16]{1,0:T(1,128)S(1)}, f32[1,16]{1,0:T(1,128)}, u32[]{:S(2)}) copy-start(f32[1,16]{1,0:T(1,128)} %param.7) | copy-start | bytes 196
  160.2 2.0 %copy-start.2 = (f32[2,8,128,256]{3,2,1,0:T(8,128)S(1)}, f32[2,8,128,256]{3,2,1,0:T(8,128)}, u32[]{:S(2)}) copy-start(f32[2,8,128,256]{3,2,1,0:T(8,128)} %copy.100) | copy-start | bytes 6291460
where the time goes:
time: 167 us; the launch traced here: 166 us
  starting transfers between devices  67.1 us (40%)
  waiting for transfers between devices  56.8 us (34%)
  local copies, waits for them, and re-layouts  17.7 us (11%)
  matrix products  14.5 us (9%)
  other arithmetic  7.49 us (4%)
  blocking collectives  2.26 us (1%)
    all_to_all x2, starting transfers between devices, sent_together(): lax.all_to_all(both, axis, split_axis=split_dim, concat_axis=concat_dim,...  63.3 us
    all_to_all x2, waiting for transfers between devices, sent_together(): lax.all_to_all(both, axis, split_axis=split_dim, concat_axis=concat_dim,...  56.8 us
    unnamed x23, local copies, waits for them, and re-layouts  10.1 us
    unnamed x2, other arithmetic  5.07 us
    dot_general x1, matrix products, z_inverse(): jnp.dot(joined, inverse_z, precision=HIGHEST).reshape(outer, rows_count, NZ)  4.1 us
    all_to_all x1, starting transfers between devices, copy_for_each(): lax.all_to_all(jnp.broadcast_to(value[None], (size, *value.shape)), axis,...  3.79 us
  transfers between devices with their start and end apart: 3, of which 2 were waited for; matrix products, arithmetic and copies ran while one was open for 12% of the time, Pallas kernels for 0%

commit v1 on v0

v1 whole, which is shorter than its diff:
```python
import functools

import jax
import jax.numpy as jnp
import ml_dtypes
import numpy as np
from jax import lax
from jax.experimental import pallas as pl
from jax.experimental.pallas import tpu as pltpu
from jax.sharding import PartitionSpec as P

C = 32
NX = 128
NY = 128
NZ = 256
MX = 16
MY = 32
MZ = 32
KB = 4
K8 = 8
LC = 16

F32 = jnp.float32
BF16 = jnp.bfloat16


def tables(length, kept_count):
    offsets = np.arange(kept_count)
    freqs = np.where(offsets < kept_count // 2, offsets, length - kept_count + offsets)
    angles = (freqs[:, None] * np.arange(length)[None, :] % length) * (2.0 * np.pi / length)
    return np.cos(angles), np.sin(angles)


def halves(table):
    table = np.asarray(table, np.float32)
    high = table.astype(ml_dtypes.bfloat16)
    low = (table - high.astype(np.float32)).astype(ml_dtypes.bfloat16)
    return high, low


@functools.cache
def constants():
    cos_x, sin_x = tables(NX, MX)
    cos_y, sin_y = tables(NY, MY)
    cos_z, sin_z = tables(NZ, MZ)
    tz = np.concatenate(halves(np.concatenate([cos_z, -sin_z], 0) * NZ**-0.5), 0)
    wy = np.concatenate([np.concatenate([cos_y, sin_y], 1), np.concatenate([-sin_y, cos_y], 1)], 0)
    wy = np.concatenate(halves(wy * NY**-0.5), 0)
    wx = np.concatenate([np.stack([cos_x, sin_x], 2), np.stack([-sin_x, cos_x], 2)], 0).reshape(2 * MX, 2 * NX)
    wx = np.concatenate(halves(wx * NX**-0.5), 0)
    vx = np.stack([np.concatenate([cos_x, -sin_x], 0).T, np.concatenate([sin_x, cos_x], 0).T], 1)
    high, low = halves(vx.reshape(2 * NX, 2 * MX) * MX**-0.5)
    vx = np.concatenate([high, low, high], 1)
    vy = np.concatenate([np.concatenate([cos_y, sin_y], 1), np.concatenate([-sin_y, cos_y], 1)], 0)
    vy = np.stack(halves(vy * MY**-0.5), 0)
    vz = np.stack(halves(np.concatenate([cos_z, -sin_z], 0) * MZ**-0.5), 0)
    return tz, wy, wx, vx, vy, vz


def split(value):
    high = value.astype(BF16)
    return high, (value - high.astype(F32)).astype(BF16)


def dot(a, b, dims=((1,), (0,))):
    return lax.dot_general(a, b, (dims, ((), ())), preferred_element_type=F32)


STEPS = 4


def forward_kernel(f_ref, tz_ref, wy_ref, o_ref, z_ref):
    step = pl.program_id(0)
    per = LC // STEPS
    for n in range(per):
        rows = dot(tz_ref[...], f_ref[n], ((1,), (1,)))
        rows = rows[: 2 * MZ] + rows[2 * MZ :]
        at = pl.multiple_of((step * per + n) * K8, K8)
        for part in range(2):
            for b in range(KB):
                lo = part * MZ + b * K8
                z_ref[b, pl.ds(at, K8), part * NY : (part + 1) * NY] = rows[lo : lo + K8]

    @pl.when(step == STEPS - 1)
    def _():
        for b in range(KB):
            high, low = split(z_ref[b])
            out = dot(wy_ref[...], high, ((1,), (1,)))
            out = out[: 2 * MY] + out[2 * MY :] + dot(wy_ref[: 2 * MY], low, ((1,), (1,)))
            for part in range(2):
                o_ref[pl.ds(2 * b + part, MY, stride=2 * KB), :] = out[part * MY : (part + 1) * MY]


def forward(field, tz, wy):
    per = LC // STEPS
    return pl.pallas_call(
        forward_kernel,
        grid=(STEPS,),
        in_specs=[
            pl.BlockSpec((per, NY, NZ), lambda s: (s, 0, 0)),
            pl.BlockSpec(tz.shape, lambda s: (0, 0)),
            pl.BlockSpec(wy.shape, lambda s: (0, 0)),
        ],
        out_specs=pl.BlockSpec((2 * MY * KB, LC * K8), lambda s: (0, 0)),
        out_shape=jax.ShapeDtypeStruct((2 * MY * KB, LC * K8), F32),
        scratch_shapes=[pltpu.VMEM((KB, LC * K8, 2 * NY), F32)],
        name="forward",
    )(field, tz, wy)


def x_forward_kernel(s_ref, wx_ref, o_ref):
    high, low = split(s_ref[...])
    out = dot(wx_ref[...], high)
    o_ref[...] = out[: 2 * MX] + out[2 * MX :] + dot(wx_ref[: 2 * MX], low)


def x_forward(sent, wx):
    return pl.pallas_call(
        x_forward_kernel,
        out_shape=jax.ShapeDtypeStruct((2 * MX, LC * K8), F32),
        name="x_forward",
    )(sent, wx)


def mix_kernel(x_ref, w_ref, vx_ref, o_ref):
    lanes = LC * K8
    within = lax.broadcasted_iota(jnp.int32, (MX, lanes), 1) % K8
    real_g = jnp.zeros((MX, lanes), F32)
    imag_g = jnp.zeros((MX, lanes), F32)
    for i in range(C):
        at = within + (i % LC) * K8
        real = jnp.take_along_axis(x_ref[i // LC, :MX], at, axis=1)
        imag = jnp.take_along_axis(x_ref[i // LC, MX:], at, axis=1)
        w_re = w_ref[0, i].astype(F32)
        w_im = w_ref[1, i].astype(F32)
        real_g += w_re * real - w_im * imag
        imag_g += w_re * imag + w_im * real
    high, low = split(jnp.concatenate([real_g, imag_g], 0))
    o_ref[...] = dot(vx_ref[...], jnp.concatenate([high, high, low], 0))


def mix(both, weights, vx):
    return pl.pallas_call(
        mix_kernel,
        out_shape=jax.ShapeDtypeStruct((2 * NX, LC * K8), F32),
        name="mix",
    )(both, weights, vx)


BYPASS_ROWS = 16


def bypass_kernel(w_ref, bias_ref, f_ref, g_ref, o_ref):
    rows = LC * BYPASS_ROWS
    total = bias_ref[...]
    for n, ref in enumerate((f_ref, g_ref)):
        high, low = split(w_ref[:, n * rows : (n + 1) * rows])
        block = ref[...].reshape(rows, NZ)
        total = total + (dot(high, block) + dot(low, block))
    o_ref[...] = total.reshape(LC, BYPASS_ROWS, NZ)


def bypass_of(weights, bias, own, other):
    block = pl.BlockSpec((LC, BYPASS_ROWS, NZ), lambda s: (0, s, 0))
    return pl.pallas_call(
        bypass_kernel,
        grid=(NY // BYPASS_ROWS,),
        in_specs=[
            pl.BlockSpec(weights.shape, lambda s: (0, 0)),
            pl.BlockSpec(bias.shape, lambda s: (0, 0)),
            block,
            block,
        ],
        out_specs=block,
        out_shape=jax.ShapeDtypeStruct((LC, NY, NZ), F32),
        name="bypass",
    )(weights, bias, own, other)


def inverse_kernel(h_ref, vy_ref, vz_ref, b_ref, f_ref, o_ref, a_ref):
    o = pl.program_id(0)

    @pl.when(o == 0)
    def _():
        for b in range(KB):
            parts = [h_ref[pl.ds(2 * b + part, MY, stride=2 * KB), :] for part in range(2)]
            high, low = split(jnp.concatenate(parts, 0).T)
            a_ref[b] = dot(high, vy_ref[0]) + dot(low, vy_ref[0]) + dot(high, vy_ref[1])

    at = pl.multiple_of(o * K8, K8)
    parts = [
        a_ref[b, pl.ds(at, K8), part * NY : (part + 1) * NY] for part in range(2) for b in range(KB)
    ]
    high, low = split(jnp.concatenate(parts, 0).T)
    value = dot(high, vz_ref[0]) + dot(low, vz_ref[0]) + dot(high, vz_ref[1]) + b_ref[0]
    gelu = 0.5 * value * (1.0 + jnp.tanh(np.sqrt(2.0 / np.pi) * (value + 0.044715 * value * value * value)))
    o_ref[0] = f_ref[0].astype(F32) + gelu


def inverse(sent, vy, vz, pre, field):
    block = pl.BlockSpec((1, NY, NZ), lambda s: (s, 0, 0))
    return pl.pallas_call(
        inverse_kernel,
        grid=(LC,),
        in_specs=[
            pl.BlockSpec((2 * MY * KB, LC * K8), lambda s: (0, 0)),
            pl.BlockSpec(vy.shape, lambda s: (0, 0, 0)),
            pl.BlockSpec(vz.shape, lambda s: (0, 0, 0)),
            block,
            block,
        ],
        out_specs=block,
        out_shape=jax.ShapeDtypeStruct((LC, NY, NZ), F32),
        scratch_shapes=[pltpu.VMEM((KB, LC * K8, 2 * NY), F32)],
        name="inverse",
    )(sent, vy, vz, pre, field)


def exchange(value):
    sent = lax.all_to_all(value.reshape(NX, 2, LC * K8), "pen", 0, 0, tiled=True)
    return sent.reshape(2 * NX, LC * K8)


def local(features, spectral_weights, bypass_weights, bypass_bias):
    tz, wy, wx, vx, vy, vz = constants()
    field = features[0]
    other = lax.ppermute(field, "ch", [(0, 1), (1, 0)])

    modes = exchange(forward(field, tz, wy))

    weights = spectral_weights[0].transpose(0, 2, 1, 3, 4).reshape(2, C, MX, LC * K8)

    core = lax.axis_index("ch")
    mixing = bypass_weights[0].reshape(2, LC, LC)
    mixing = jnp.where(core == 0, mixing, mixing[::-1]).reshape(C, LC)
    eye = jnp.eye(BYPASS_ROWS, dtype=F32)
    spread = mixing.T[:, None, :, None] * eye[None, :, None, :]
    spread = spread.reshape(LC * BYPASS_ROWS, C * BYPASS_ROWS)
    offsets = jnp.repeat(bypass_bias[0], BYPASS_ROWS)[:, None]
    pre = bypass_of(spread, offsets, field, other)

    both = lax.all_gather(x_forward(modes, wx), "ch")
    back = exchange(mix(both, weights, vx))
    return inverse(back, vy, vz, pre, field)[None]


def solution(mesh):
    return jax.shard_map(
        local,
        mesh=mesh,
        in_specs=(
            P(("grp", "pen"), "ch", None, None),
            P(None, None, None, None, "ch", "pen"),
            P(None, None, "ch"),
            P(None, "ch"),
        ),
        out_specs=P(("grp", "pen"), "ch", None, None),
        check_vma=False,
    )
```

time: 167 us -> 149 us (0.89)
  Pallas kernels: 0 us -> 26.4 us
  waiting for transfers between devices: 56.8 us -> 39.6 us
  matrix products: 14.5 us -> 0 us
  local copies, waits for them, and re-layouts: 17.7 us -> 11.4 us
  other arithmetic: 7.49 us -> 2.55 us
  starting transfers between devices: 67.1 us -> 65 us
    pallas_call x0 -> x5, Pallas kernels: none -> 26.4 us  [the longest x1 12 us: inverse(): pl.pallas_call(inverse_kernel, grid=(LC,), in_specs=[pl.BlockSpec((2 * MY...]
    all_to_all x3 -> x2, waiting for transfers between devices: 56.8 us -> 39.6 us  [exchange(): lax.all_to_all(value.reshape(NX, 2, LC * K8), 'pen', 0, 0, tiled=True)]
    dot_general x19 -> x0, matrix products: 14.5 us -> none  [the longest x1 4.1 us: z_inverse(): jnp.dot(joined, inverse_z, precision=HIGHEST).reshape(outer, rows_count, NZ)]
    unnamed x23 -> x8, local copies, waits for them, and re-layouts: 10.1 us -> 2.27 us
    unnamed x2 -> x0, other arithmetic: 5.07 us -> none
    mul x2 -> x1, local copies, waits for them, and re-layouts: 0.26 us -> 5.12 us  [local(): spread = mixing.T[:, None, :, None] * eye[None, :, None, :]]
    all_to_all x3 -> x2, starting transfers between devices: 67.1 us -> 63.1 us  [exchange(): lax.all_to_all(value.reshape(NX, 2, LC * K8), 'pen', 0, 0, tiled=True)]
    mul x0 -> x1, other arithmetic: none -> 2.54 us  [local(): spread = mixing.T[:, None, :, None] * eye[None, :, None, :]]
  transfers between devices with their start and end apart: 3 -> 3, of which waited for: 2 -> 2; matrix products, arithmetic and copies ran while one was open for 12% -> 8% of each run, Pallas kernels for 0% -> 7%
where the time goes in v1:
time: 149 us; the launch traced here: 148 us
  starting transfers between devices  65 us (44%)
  waiting for transfers between devices  39.6 us (27%)
  Pallas kernels  26.4 us (18%)
  local copies, waits for them, and re-layouts  11.4 us (8%)
  blocking collectives  3.16 us (2%)
  other arithmetic  2.55 us (2%)
    all_to_all x2, starting transfers between devices, exchange(): lax.all_to_all(value.reshape(NX, 2, LC * K8), 'pen', 0, 0, tiled=True)  63.1 us
    all_to_all x2, waiting for transfers between devices, exchange(): lax.all_to_all(value.reshape(NX, 2, LC * K8), 'pen', 0, 0, tiled=True)  39.6 us
    pallas_call x1, Pallas kernels, inverse(): pl.pallas_call(inverse_kernel, grid=(LC,), in_specs=[pl.BlockSpec((2 * MY...  12 us
    pallas_call x1, Pallas kernels, bypass_of(): pl.pallas_call(bypass_kernel, grid=(NY // BYPASS_ROWS,), in_specs=[pl.Blo...  7.11 us
    mul x1, local copies, waits for them, and re-layouts, local(): spread = mixing.T[:, None, :, None] * eye[None, :, None, :]  5.12 us
    pallas_call x1, Pallas kernels, forward(): pl.pallas_call(forward_kernel, grid=(STEPS,), in_specs=[pl.BlockSpec((per...  3.59 us
    all_gather x1, blocking collectives, local(): both = lax.all_gather(x_forward(modes, wx), 'ch')  3.16 us
  transfers between devices with their start and end apart: 3, of which 2 were waited for; matrix products, arithmetic and copies ran while one was open for 8% of the time, Pallas kernels for 7%

profile of v1, /device:TPU:40, one launch (start us, length us, event | category | flops | bytes accessed | tf_op | source)
XLA Modules:
  0.0 148.2 jit_solution(4838648722270126626)
XLA Ops:
  0.0 3.6 %forward.1 = f32[256,128]{1,0:T(8,128)} custom-call(bf16[16,128,256]{2,1,0:T(8,128)(2,1)} %bitcast.23, bf16[128,256]{1,0:T(8,128)(2,1)} %constant.18.clone.tz_ref, bf16[128,256]{1,0:T(8,128)(2,1)} %constant.19.clone.wy_ref), custom_call_target="tpu_custom_call" | custom-call | tf_op jit(solution)/shard_map/forward/pallas_call | solution.py:96
  3.6 53.2 %all-to-all-start = ((f32[128,2,128]{2,1,0:T(2,128)}), f32[128,2,128]{2,1,0:T(2,128)S(1)}, u32[]{:S(2)}, u32[]{:S(2)}) async-start(f32[128,2,128]{2,1,0:T(2,128)} %bitcast.29), calls=%async_computation | async-start | bytes 262144 | tf_op jit(solution)/shard_map/all_to_all | solution.py:220
  56.8 2.0 %collective-permute-start = (bf16[16,128,256]{2,1,0:T(8,128)(2,1)}, bf16[16,128,256]{2,1,0:T(8,128)(2,1)S(1)}, u32[]{:S(2)}, u32[]{:S(2)}) collective-permute-start(bf16[16,128,256]{2,1,0:T(8,128)(2,1)} %bitcast.24), channel_id=1, source_target_pairs={{0,1},{1,0},{2,3},{3,2},{4,5},{5,4},{6,7},{7,6},{8,9},{9,8},{10,11... | collective-permute-start | bytes 3145736 | tf_op jit(solution)/shard_map/ppermute | solution.py:227
  58.7 2.3 %copy.12.w_ref = bf16[2,32,16,128]{3,2,1,0:T(8,128)(2,1)} copy(bf16[2,32,16,128]{1,3,2,0:T(8,128)(2,1)} %bitcast.27) | data formatting | bytes 524288 | tf_op jit(solution)/shard_map/reshape | solution.py:231
  61.0 26.1 %all-to-all-done = f32[128,2,128]{2,1,0:T(2,128)S(1)} async-done(((f32[128,2,128]{2,1,0:T(2,128)}), f32[128,2,128]{2,1,0:T(2,128)S(1)}, u32[]{:S(2)}, u32[]{:S(2)}) %all-to-all-start) | async-done | bytes 131104 | tf_op jit(solution)/shard_map/all_to_all | solution.py:220
  87.1 0.0 copy-start.2
  87.1 0.6 copy-done.2
  87.8 1.7 %x_forward.1 = f32[32,128]{1,0:T(8,128)} custom-call(f32[256,128]{1,0:T(8,128)} %bitcast.30, bf16[64,256]{1,0:T(8,128)(2,1)} %constant.20.clone.wx_ref), custom_call_target="tpu_custom_call" | custom-call | tf_op jit(solution)/shard_map/x_forward/pallas_call | solution.py:118
  89.4 3.2 %all-gather = f32[64,128]{1,0:T(8,128)} all-gather(f32[32,128]{1,0:T(8,128)} %x_forward.1), channel_id=2, replica_groups=mesh['grp'=2,'pen'=128,'ch'=2] {'ch'}, dimensions={0}, use_global_device_ids=true | all-gather | bytes 49152 | tf_op jit(solution)/shard_map/all_gather | solution.py:242
  92.6 2.1 %mix.1 = f32[256,128]{1,0:T(8,128)} custom-call(f32[2,32,128]{2,1,0:T(8,128)} %bitcast.33, bf16[2,32,16,128]{3,2,1,0:T(8,128)(2,1)} %copy.12.w_ref, bf16[256,96]{1,0:T(8,128)(2,1)} %constant.21.clone.vx_ref), custom_call_target="tpu_custom_call" | custom-call | tf_op jit(solution)/shard_map/mix/pallas_call | solution.py:143
  94.7 9.9 %all-to-all-start.1 = ((f32[128,2,128]{2,1,0:T(2,128)}), f32[128,2,128]{2,1,0:T(2,128)S(1)}, u32[]{:S(2)}, u32[]{:S(2)}) async-start(f32[128,2,128]{2,1,0:T(2,128)} %bitcast.31), calls=%async_computation.1 | async-start | bytes 262144 | tf_op jit(solution)/shard_map/all_to_all | solution.py:220
  104.6 0.8 reshape_squeeze.3
  105.4 0.1 reshape.36
  105.5 0.0 copy-start.3
  105.5 2.5 %broadcast_multiply_fusion = f32[16,16,32,16]{3,2,1,0:T(8,128)} fusion(f32[16,16]{1,0:T(8,128)S(1)} %fusion, f32[16,32]{1,0:T(8,128)S(1)} %bitcast.36), kind=kLoop, calls=%fused_computation | loop fusion | flops 131072 | bytes 527360 | tf_op jit(solution)/shard_map/mul | solution.py:237
  108.0 5.1 %mul.20.w_ref = f32[256,512]{1,0:T(8,128)} reshape(f32[16,16,32,16]{3,2,1,0:T(8,128)} %broadcast_multiply_fusion) | data formatting | bytes 1048576 | tf_op jit(solution)/shard_map/mul | solution.py:237
  113.2 0.0 copy-done.3
  113.2 0.1 broadcast_in_dim.8
  113.2 0.8 broadcast_in_dim_reshape.4.bias_ref
  114.0 0.0 collective-permute-done.g_ref
  114.0 0.0 copy-start
  114.0 1.0 copy-done
  115.0 7.1 %bypass.1.b_ref = f32[16,128,256]{2,1,0:T(8,128)} custom-call(f32[256,512]{1,0:T(8,128)} %mul.20.w_ref, f32[256,1]{1,0:T(8,128)} %broadcast_in_dim_reshape.4.bias_ref, bf16[16,128,256]{2,1,0:T(8,128)(2,1)} %bitcast.25, bf16[16,128,256]{2,1,0:T(8,128)(2,1)} %copy-done), custom_call_target="tpu_custom_call" | custom-call | tf_op jit(solution)/shard_map/bypass/pallas_call | solution.py:165
  122.1 13.5 %all-to-all-done.1 = f32[128,2,128]{2,1,0:T(2,128)S(1)} async-done(((f32[128,2,128]{2,1,0:T(2,128)}), f32[128,2,128]{2,1,0:T(2,128)S(1)}, u32[]{:S(2)}, u32[]{:S(2)}) %all-to-all-start.1) | async-done | bytes 131104 | tf_op jit(solution)/shard_map/all_to_all | solution.py:220
  135.6 0.0 copy-start.1
  135.6 0.6 copy-done.1
  136.3 12.0 %inverse.1 = f32[16,128,256]{2,1,0:T(8,128)} custom-call(f32[256,128]{1,0:T(8,128)} %bitcast.28, bf16[2,64,256]{2,1,0:T(8,128)(2,1)} %constant.22.clone.vy_ref, bf16[2,64,256]{2,1,0:T(8,128)(2,1)} %constant.23.clone.vz_ref, f32[16,128,256]{2,1,0:T(8,128)} %bypass.1.b_ref, bf16[16,128,256]{2,1,0:T(8,128)(2,1)} %bitcast.26), custom_call_target="tpu_custom_call" | custom-call | tf_op jit(solution)/shard_map/inverse/pallas_call | solution.py:202
  (3 shorter events, 0.1 us)
Async XLA Ops:
  3.6 83.5 %all-to-all-start = ((f32[128,2,128]{2,1,0:T(2,128)}), f32[128,2,128]{2,1,0:T(2,128)S(1)}, u32[]{:S(2)}, u32[]{:S(2)}) async-start(f32[128,2,128]{2,1,0:T(2,128)} %bitcast.29), calls=%async_computation | async-start | bytes 262144 | tf_op jit(solution)/shard_map/all_to_all | solution.py:220
  56.8 57.2 %collective-permute-start = (bf16[16,128,256]{2,1,0:T(8,128)(2,1)}, bf16[16,128,256]{2,1,0:T(8,128)(2,1)S(1)}, u32[]{:S(2)}, u32[]{:S(2)}) collective-permute-start(bf16[16,128,256]{2,1,0:T(8,128)(2,1)} %bitcast.24), channel_id=1, source_target_pairs={{0,1},{1,0},{2,3},{3,2},{4,5},{5,4},{6,7},{7,6},{8,9},{9,8},{10,11... | collective-permute-start | bytes 3145736 | tf_op jit(solution)/shard_map/ppermute | solution.py:227
  87.1 0.7 copy-start.2
  94.7 41.0 %all-to-all-start.1 = ((f32[128,2,128]{2,1,0:T(2,128)}), f32[128,2,128]{2,1,0:T(2,128)S(1)}, u32[]{:S(2)}, u32[]{:S(2)}) async-start(f32[128,2,128]{2,1,0:T(2,128)} %bitcast.31), calls=%async_computation.1 | async-start | bytes 262144 | tf_op jit(solution)/shard_map/all_to_all | solution.py:220
  105.5 7.7 %copy-start.3 = (f32[1,16]{1,0:T(1,128)S(1)}, f32[1,16]{1,0:T(1,128)}, u32[]{:S(2)}) copy-start(f32[1,16]{1,0:T(1,128)} %param.13) | copy-start | bytes 196
  114.0 1.0 copy-start
  135.6 0.7 copy-start.1

commit v2 on v1

v2 whole, which is shorter than its diff:
```python
import functools

import jax
import jax.numpy as jnp
import ml_dtypes
import numpy as np
from jax import lax
from jax.experimental import pallas as pl
from jax.experimental.pallas import tpu as pltpu
from jax.sharding import Mesh, PartitionSpec as P

C = 32
NX = 128
NY = 128
NZ = 256
MX = 16
MY = 32
MZ = 32
KB = 4
K8 = 8
LC = 16
PX, PZ = 4, 32
ORDER = [(place % PX) * PZ + place // PX for place in range(PX * PZ)]

F32 = jnp.float32
BF16 = jnp.bfloat16


def tables(length, kept_count):
    offsets = np.arange(kept_count)
    freqs = np.where(offsets < kept_count // 2, offsets, length - kept_count + offsets)
    angles = (freqs[:, None] * np.arange(length)[None, :] % length) * (2.0 * np.pi / length)
    return np.cos(angles), np.sin(angles)


def halves(table):
    table = np.asarray(table, np.float32)
    high = table.astype(ml_dtypes.bfloat16)
    low = (table - high.astype(np.float32)).astype(ml_dtypes.bfloat16)
    return high, low


@functools.cache
def constants():
    cos_x, sin_x = (table[:, ORDER] for table in tables(NX, MX))
    cos_y, sin_y = tables(NY, MY)
    cos_z, sin_z = tables(NZ, MZ)
    tz = np.concatenate(halves(np.concatenate([cos_z, -sin_z], 0) * NZ**-0.5), 0)
    wy = np.concatenate([np.concatenate([cos_y, sin_y], 1), np.concatenate([-sin_y, cos_y], 1)], 0)
    wy = np.concatenate(halves(wy * NY**-0.5), 0)
    wx = np.concatenate([np.stack([cos_x, sin_x], 2), np.stack([-sin_x, cos_x], 2)], 0).reshape(2 * MX, 2 * NX)
    wx = np.concatenate(halves(wx * NX**-0.5), 0)
    vx = np.stack([np.concatenate([cos_x, -sin_x], 0).T, np.concatenate([sin_x, cos_x], 0).T], 1)
    high, low = halves(vx.reshape(2 * NX, 2 * MX) * MX**-0.5)
    vx = np.concatenate([high, low, high], 1)
    vy = np.concatenate([np.concatenate([cos_y, sin_y], 1), np.concatenate([-sin_y, cos_y], 1)], 0)
    vy = np.stack(halves(vy * MY**-0.5), 0)
    vz = np.stack(halves(np.concatenate([cos_z, -sin_z], 0) * MZ**-0.5), 0)
    return tz, wy, wx, vx, vy, vz


def split(value):
    high = value.astype(BF16)
    return high, (value - high.astype(F32)).astype(BF16)


def rows_of(b, n, part):
    return pl.ds(2 * PX * b + 2 * n + part, 8, stride=2 * PX * KB)


def dot(a, b, dims=((1,), (0,))):
    return lax.dot_general(a, b, (dims, ((), ())), preferred_element_type=F32)


STEPS = 4
VMEM = pl.BlockSpec(memory_space=pltpu.VMEM)
PARAMS = pltpu.CompilerParams(vmem_limit_bytes=16 << 20)


def near(*values):
    return tuple(pltpu.with_memory_space_constraint(v, pltpu.VMEM) for v in values)


def forward_kernel(f_ref, tz_ref, wy_ref, o_ref, z_ref):
    step = pl.program_id(0)
    per = LC // STEPS
    for n in range(per):
        rows = dot(tz_ref[...], f_ref[n], ((1,), (1,)))
        rows = rows[: 2 * MZ] + rows[2 * MZ :]
        at = pl.multiple_of((step * per + n) * K8, K8)
        for part in range(2):
            for b in range(KB):
                lo = part * MZ + b * K8
                z_ref[b, pl.ds(at, K8), part * NY : (part + 1) * NY] = rows[lo : lo + K8]

    @pl.when(step == STEPS - 1)
    def _():
        for b in range(KB):
            high, low = split(z_ref[b])
            out = dot(wy_ref[...], high, ((1,), (1,)))
            out = out[: 2 * MY] + out[2 * MY :] + dot(wy_ref[: 2 * MY], low, ((1,), (1,)))
            for part in range(2):
                for n in range(PX):
                    lo = part * MY + n * 8
                    o_ref[rows_of(b, n, part), :] = out[lo : lo + 8]


def forward(field, tz, wy):
    per = LC // STEPS
    return pl.pallas_call(
        forward_kernel,
        grid=(STEPS,),
        in_specs=[
            pl.BlockSpec((per, NY, NZ), lambda s: (s, 0, 0)),
            pl.BlockSpec(tz.shape, lambda s: (0, 0)),
            pl.BlockSpec(wy.shape, lambda s: (0, 0)),
        ],
        out_specs=VMEM,
        out_shape=pltpu.VMEM((2 * MY * KB, LC * K8), F32),
        scratch_shapes=[pltpu.VMEM((KB, LC * K8, 2 * NY), F32)],
        name="forward",
        compiler_params=PARAMS,
    )(*(pltpu.with_memory_space_constraint(v, pltpu.HBM) for v in (field, jnp.asarray(tz), jnp.asarray(wy))))


def x_forward_kernel(s_ref, wx_ref, o_ref):
    high, low = split(s_ref[...])
    out = dot(wx_ref[...], high)
    o_ref[...] = out[: 2 * MX] + out[2 * MX :] + dot(wx_ref[: 2 * MX], low)


def x_forward(sent, wx):
    return pl.pallas_call(
        x_forward_kernel,
        in_specs=[VMEM] * 2,
        out_specs=VMEM,
        out_shape=pltpu.VMEM((2 * MX, LC * K8), F32),
        name="x_forward",
        compiler_params=PARAMS,
    )(*near(sent, wx))


def mix_kernel(x_ref, w_ref, vx_ref, o_ref):
    lanes = LC * K8
    within = lax.broadcasted_iota(jnp.int32, (MX, lanes), 1) % K8
    real_g = jnp.zeros((MX, lanes), F32)
    imag_g = jnp.zeros((MX, lanes), F32)
    for i in range(C):
        at = within + (i % LC) * K8
        real = jnp.take_along_axis(x_ref[i // LC, :MX], at, axis=1)
        imag = jnp.take_along_axis(x_ref[i // LC, MX:], at, axis=1)
        w_re = w_ref[0, i].astype(F32)
        w_im = w_ref[1, i].astype(F32)
        real_g += w_re * real - w_im * imag
        imag_g += w_re * imag + w_im * real
    high, low = split(jnp.concatenate([real_g, imag_g], 0))
    o_ref[...] = dot(vx_ref[...], jnp.concatenate([high, high, low], 0))


def mix(both, weights, vx):
    return pl.pallas_call(
        mix_kernel,
        in_specs=[VMEM] * 3,
        out_specs=VMEM,
        out_shape=pltpu.VMEM((2 * NX, LC * K8), F32),
        name="mix",
        compiler_params=PARAMS,
    )(*near(both, weights, vx))


BYPASS_ROWS = 16


def bypass_kernel(core_ref, bias_ref, w_ref, f_ref, g_ref, vy_in, vz_in, o_ref, vy_ref, vz_ref, w2_ref):
    rows = LC * BYPASS_ROWS
    step = pl.program_id(0)

    @pl.when(step == 0)
    def _():
        row_of = lax.broadcasted_iota(jnp.int32, (rows, LC), 0) // BYPASS_ROWS
        left = (row_of == lax.broadcasted_iota(jnp.int32, (rows, LC), 1)).astype(BF16)
        same = (
            lax.broadcasted_iota(jnp.int32, (rows, rows), 0) % BYPASS_ROWS
            == lax.broadcasted_iota(jnp.int32, (rows, rows), 1) % BYPASS_ROWS
        )
        col_of = lax.broadcasted_iota(jnp.int32, (C, rows), 1) // BYPASS_ROWS
        channel = lax.broadcasted_iota(jnp.int32, (C, rows), 0)
        core = core_ref[0]
        for n, part in enumerate(split(w_ref[...])):
            tall = dot(left, part).astype(BF16)
            for k in range(2):
                first = LC * (core if k == 0 else 1 - core)
                pick = (channel == col_of + first).astype(BF16)
                w2_ref[k, n] = jnp.where(same, dot(tall, pick), 0.0).astype(BF16)
        vy_ref[...] = vy_in[...]
        vz_ref[...] = vz_in[...]

    at = pl.multiple_of(step * BYPASS_ROWS, BYPASS_ROWS)
    total = None
    for k, ref in enumerate((f_ref, g_ref)):
        block = (ref[:, pl.ds(at, BYPASS_ROWS), :] if k == 0 else ref[...]).reshape(rows, NZ)
        term = dot(w2_ref[k, 0], block) + dot(w2_ref[k, 1], block)
        total = term if total is None else total + term
    for o in range(LC):
        o_ref[o, pl.ds(at, BYPASS_ROWS), :] = total[o * BYPASS_ROWS : (o + 1) * BYPASS_ROWS] + bias_ref[0, o]


def bypass_of(core, bias, weights, own, other, vy, vz):
    rows = LC * BYPASS_ROWS
    smem = pl.BlockSpec(memory_space=pltpu.SMEM)
    whole = pl.BlockSpec(weights.shape, lambda s: (0, 0))
    return pl.pallas_call(
        bypass_kernel,
        grid=(NY // BYPASS_ROWS,),
        in_specs=[smem, smem, whole, VMEM, pl.BlockSpec((LC, BYPASS_ROWS, NZ), lambda s: (0, s, 0))]
        + [pl.BlockSpec(v.shape, lambda s: (0, 0, 0)) for v in (vy, vz)],
        out_specs=[VMEM] * 3,
        out_shape=[pltpu.VMEM((LC, NY, NZ), F32), pltpu.VMEM(vy.shape, BF16), pltpu.VMEM(vz.shape, BF16)],
        scratch_shapes=[pltpu.VMEM((2, 2, rows, rows), BF16)],
        name="bypass",
        compiler_params=PARAMS,
    )(core, bias, weights, *near(own), other, vy, vz)


def stage_kernel(wx_in, vx_in, wx_ref, vx_ref):
    wx_ref[...] = wx_in[...]
    vx_ref[...] = vx_in[...]


def stage(wx, vx):
    return pl.pallas_call(
        stage_kernel,
        out_specs=[VMEM] * 2,
        out_shape=[pltpu.VMEM(wx.shape, BF16), pltpu.VMEM(vx.shape, BF16)],
        name="stage",
        compiler_params=PARAMS,
    )(wx, vx)


INVERSE_STEPS = 4


def inverse_kernel(h_ref, vy_ref, vz_ref, b_ref, f_ref, o_ref, a_ref):
    step = pl.program_id(0)
    per = LC // INVERSE_STEPS

    @pl.when(step == 0)
    def _():
        for b in range(KB):
            parts = [h_ref[rows_of(b, n, part), :] for part in range(2) for n in range(PX)]
            high, low = split(jnp.concatenate(parts, 0).T)
            a_ref[b] = dot(high, vy_ref[0]) + dot(low, vy_ref[0]) + dot(high, vy_ref[1])

    for n in range(per):
        o = step * per + n
        at = pl.multiple_of(o * K8, K8)
        parts = [
            a_ref[b, pl.ds(at, K8), part * NY : (part + 1) * NY] for part in range(2) for b in range(KB)
        ]
        high, low = split(jnp.concatenate(parts, 0).T)
        value = dot(high, vz_ref[0]) + dot(low, vz_ref[0]) + dot(high, vz_ref[1]) + b_ref[o]
        gelu = 0.5 * value * (1.0 + jnp.tanh(np.sqrt(2.0 / np.pi) * (value + 0.044715 * value * value * value)))
        o_ref[n] = f_ref[o].astype(F32) + gelu


def inverse(sent, vy, vz, pre, field):
    return pl.pallas_call(
        inverse_kernel,
        grid=(INVERSE_STEPS,),
        in_specs=[VMEM] * 5,
        out_specs=pl.BlockSpec((LC // INVERSE_STEPS, NY, NZ), lambda s: (s, 0, 0)),
        out_shape=jax.ShapeDtypeStruct((LC, NY, NZ), F32),
        scratch_shapes=[pltpu.VMEM((KB, LC * K8, 2 * NY), F32)],
        name="inverse",
        compiler_params=PARAMS,
    )(*near(sent, vy, vz, pre, field))


def exchange(value):
    sent = lax.all_to_all(value.reshape(NX, 2, LC * K8), ("pz", "px"), 0, 0, tiled=True)
    return sent.reshape(2 * NX, LC * K8)


def local(features, spectral_weights, bypass_weights, bypass_bias):
    tz, wy, wx, vx, vy, vz = constants()
    field = features[0]
    other = lax.ppermute(field, "ch", [(0, 1), (1, 0)])

    modes = exchange(forward(field, tz, wy))

    weights = spectral_weights[0].transpose(0, 2, 1, 3, 4).reshape(2, C, MX, LC * K8)

    core = lax.axis_index("ch").astype(jnp.int32)[None]
    pre, vy, vz = bypass_of(core, bypass_bias, bypass_weights[0].T, field, other, vy, vz)

    wx, vx = stage(wx, vx)
    both = lax.all_gather(x_forward(modes, wx), "ch")
    back = exchange(mix(both, weights, vx))
    return inverse(back, vy, vz, pre, field)[None]


def solution(mesh):
    groups, _, cores = mesh.devices.shape
    chips = Mesh(mesh.devices.reshape(groups, PX, PZ, cores), ("grp", "px", "pz", "ch"))
    return jax.shard_map(
        local,
        mesh=chips,
        in_specs=(
            P(("grp", "px", "pz"), "ch", None, None),
            P(None, None, None, None, "ch", ("px", "pz")),
            P(None, None, "ch"),
            P(None, "ch"),
        ),
        out_specs=P(("grp", "px", "pz"), "ch", None, None),
        check_vma=False,
    )
```

time: 149 us -> 130 us (0.87)
  Pallas kernels: 26.4 us -> 12.3 us
  local copies, waits for them, and re-layouts: 11.4 us -> 3.82 us
  waiting for transfers between devices: 39.6 us -> 44.4 us
  other arithmetic: 2.55 us -> 0 us
  starting transfers between devices: 65 us -> 66.6 us
    pallas_call x4 -> x5, Pallas kernels: 22.8 us -> 8.59 us  [the longest x1 3.79 us: bypass_of(): pl.pallas_call(bypass_kernel, grid=(NY // BYPASS_ROWS,), in_specs=[smem,...]
    mul x1 -> x0, local copies, waits for them, and re-layouts: 5.12 us -> none  [local(): spread = mixing.T[:, None, :, None] * eye[None, :, None, :]]
    all_to_all x2, waiting for transfers between devices: 39.6 us -> 44.4 us  [exchange(): lax.all_to_all(value.reshape(NX, 2, LC * K8), ('pz', 'px'), 0, 0, tiled=T...]
    mul x1 -> x0, other arithmetic: 2.54 us -> none  [local(): spread = mixing.T[:, None, :, None] * eye[None, :, None, :]]
    another operation x2 -> x0, local copies, waits for them, and re-layouts: 1.53 us -> none  [the longest x1 0.78 us: local(): mixing = bypass_weights[0].reshape(2, LC, LC)]
    all_to_all x2, starting transfers between devices: 63.1 us -> 64.6 us  [exchange(): lax.all_to_all(value.reshape(NX, 2, LC * K8), ('pz', 'px'), 0, 0, tiled=T...]
  transfers between devices with their start and end apart: 3 -> 3, of which waited for: 2 -> 2; matrix products, arithmetic and copies ran while one was open for 8% -> 1% of each run, Pallas kernels for 7% -> 4%
where the time goes in v2:
time: 130 us; the launch traced here: 129 us
  starting transfers between devices  66.6 us (51%)
  waiting for transfers between devices  44.4 us (34%)
  Pallas kernels  12.3 us (9%)
  local copies, waits for them, and re-layouts  3.82 us (3%)
  blocking collectives  1.88 us (1%)
    all_to_all x2, starting transfers between devices, exchange(): lax.all_to_all(value.reshape(NX, 2, LC * K8), ('pz', 'px'), 0, 0, tiled=T...  64.6 us
    all_to_all x2, waiting for transfers between devices, exchange(): lax.all_to_all(value.reshape(NX, 2, LC * K8), ('pz', 'px'), 0, 0, tiled=T...  44.4 us
    pallas_call x1, Pallas kernels, bypass_of(): pl.pallas_call(bypass_kernel, grid=(NY // BYPASS_ROWS,), in_specs=[smem,...  3.79 us
    pallas_call x1, Pallas kernels, forward(): pl.pallas_call(forward_kernel, grid=(STEPS,), in_specs=[pl.BlockSpec((per...  3.72 us
    pallas_call x1, Pallas kernels, inverse(): pl.pallas_call(inverse_kernel, grid=(INVERSE_STEPS,), in_specs=[VMEM] * 5...  3.52 us
  transfers between devices with their start and end apart: 3, of which 2 were waited for; matrix products, arithmetic and copies ran while one was open for 1% of the time, Pallas kernels for 4%

profile of v2, /device:TPU:40, one launch (start us, length us, event | category | flops | bytes accessed | tf_op | source)
XLA Modules:
  0.0 129.1 jit_solution(1833876195542021903)
XLA Ops:
  0.0 0.0 copy-start.5
  0.0 0.0 copy-start.6
  0.0 0.0 copy-start.3
  0.0 0.0 copy-start.4
  0.0 0.0 copy-start
  0.0 0.0 copy-start.8
  0.0 0.0 copy-start.7
  0.1 3.7 %forward.1 = f32[256,128]{1,0:T(8,128)} custom-call(bf16[16,128,256]{2,1,0:T(8,128)(2,1)} %bitcast.16, bf16[128,256]{1,0:T(8,128)(2,1)} %constant.16.clone.tz_ref, bf16[128,256]{1,0:T(8,128)(2,1)} %constant.17.clone.wy_ref), custom_call_target="tpu_custom_call" | custom-call | tf_op jit(solution)/shard_map/forward/pallas_call | solution.py:110
  3.8 53.2 %all-to-all-start = ((f32[128,2,128]{2,1,0:T(2,128)}), f32[128,2,128]{2,1,0:T(2,128)S(1)}, u32[]{:S(2)}, u32[]{:S(2)}) async-start(f32[128,2,128]{2,1,0:T(2,128)} %bitcast.1), calls=%async_computation | async-start | bytes 262144 | tf_op jit(solution)/shard_map/all_to_all | solution.py:280
  57.0 2.0 %collective-permute-start = (bf16[16,128,256]{2,1,0:T(8,128)(2,1)}, bf16[16,128,256]{2,1,0:T(8,128)(2,1)S(1)}, u32[]{:S(2)}, u32[]{:S(2)}) collective-permute-start(bf16[16,128,256]{2,1,0:T(8,128)(2,1)} %bitcast.17), channel_id=1, source_target_pairs={{0,1},{1,0},{2,3},{3,2},{4,5},{5,4},{6,7},{7,6},{8,9},{9,8},{10,11... | collective-permute-start | bytes 3145736 | tf_op jit(solution)/shard_map/ppermute | solution.py:287
  58.9 1.6 %copy.12.w_ref = bf16[2,32,16,128]{3,2,1,0:T(8,128)(2,1)S(1)} copy(bf16[2,32,16,128]{1,3,2,0:T(8,128)(2,1)} %bitcast.24) | data formatting | bytes 524288 | tf_op jit(solution)/shard_map/reshape | solution.py:291
  60.5 0.0 copy-done.5
  60.5 0.0 copy-done.6
  60.6 23.5 %all-to-all-done = f32[128,2,128]{2,1,0:T(2,128)S(1)} async-done(((f32[128,2,128]{2,1,0:T(2,128)}), f32[128,2,128]{2,1,0:T(2,128)S(1)}, u32[]{:S(2)}, u32[]{:S(2)}) %all-to-all-start) | async-done | bytes 131104 | tf_op jit(solution)/shard_map/all_to_all | solution.py:280
  84.1 0.1 x_forward.1
  84.2 1.9 %all-gather = f32[64,128]{1,0:T(8,128)S(1)} all-gather(f32[32,128]{1,0:T(8,128)S(1)} %x_forward.1), channel_id=2, replica_groups=mesh['grp'=2,'px'=4,'pz'=32,'ch'=2] {'ch'}, dimensions={0}, use_global_device_ids=true | all-gather | bytes 49152 | tf_op jit(solution)/shard_map/all_gather | solution.py:297
  86.1 1.1 mix.1
  87.2 11.4 %all-to-all-start.1 = ((f32[128,2,128]{2,1,0:T(2,128)}), f32[128,2,128]{2,1,0:T(2,128)S(1)}, u32[]{:S(2)}, u32[]{:S(2)}) async-start(f32[128,2,128]{2,1,0:T(2,128)} %bitcast.7), calls=%async_computation.1 | async-start | bytes 262144 | tf_op jit(solution)/shard_map/all_to_all | solution.py:280
  98.7 0.0 collective-permute-done.g_ref
  98.7 0.0 copy-start.1
  98.7 1.0 copy-done.1
  99.6 0.0 copy-done.3
  99.6 0.0 copy-done.4
  99.6 0.0 copy-done
  99.6 0.0 copy-done.8
  99.6 0.0 copy-done.7
  99.7 0.0 copy-start.2
  99.7 1.2 copy-done.2
  100.9 3.8 %bypass.1 = (f32[16,128,256]{2,1,0:T(8,128)S(1)}, bf16[2,64,256]{2,1,0:T(8,128)(2,1)S(1)}, bf16[2,64,256]{2,1,0:T(8,128)(2,1)S(1)}) custom-call(s32[1]{0:T(128)} %bitcast.9.core_ref, f32[1,16]{1,0:T(1,128)S(1)} %copy-done.8, f32[16,32]{1,0:T(8,128)S(1)} %bitcast.23, bf16[16,128,256]{2,1,0:T(8,128)(2,1)S(1)} %bitcast.18, bf16[16,128,256]{2,1,0:T(8,128)(2,1)S(1)} %copy-done.2, ...), custom_call_target="tpu_custom_call" | custom-call | tf_op jit(solution)/shard_map/bypass/pallas_call | solution.py:212
  104.7 20.9 %all-to-all-done.1 = f32[128,2,128]{2,1,0:T(2,128)S(1)} async-done(((f32[128,2,128]{2,1,0:T(2,128)}), f32[128,2,128]{2,1,0:T(2,128)S(1)}, u32[]{:S(2)}, u32[]{:S(2)}) %all-to-all-start.1) | async-done | bytes 131104 | tf_op jit(solution)/shard_map/all_to_all | solution.py:280
  125.6 3.5 %inverse.1 = f32[16,128,256]{2,1,0:T(8,128)} custom-call(f32[256,128]{1,0:T(8,128)S(1)} %bitcast.20, bf16[2,64,256]{2,1,0:T(8,128)(2,1)S(1)} %get-tuple-element.12.vy_ref, bf16[2,64,256]{2,1,0:T(8,128)(2,1)S(1)} %get-tuple-element.13.vz_ref, f32[16,128,256]{2,1,0:T(8,128)S(1)} %get-tuple-element.14.b_ref, bf16[16,128,256]{2,1,0:T(8,128)(2,1)S(1)} %bitcast.19), custom_call_target="tpu_custom_call" | custom-call | tf_op jit(solution)/shard_map/inverse/pallas_call | solution.py:267
  (1 shorter events, 0.0 us)
Async XLA Ops:
  0.0 60.5 %copy-start.5 = (bf16[256,96]{1,0:T(8,128)(2,1)S(1)}, bf16[256,96]{1,0:T(8,128)(2,1)}, u32[]{:S(2)}) copy-start(bf16[256,96]{1,0:T(8,128)(2,1)} %constant.21.clone.vx_in) | copy-start | bytes 147460
  0.0 60.5 %copy-start.6 = (bf16[64,256]{1,0:T(8,128)(2,1)S(1)}, bf16[64,256]{1,0:T(8,128)(2,1)}, u32[]{:S(2)}) copy-start(bf16[64,256]{1,0:T(8,128)(2,1)} %constant.20.clone.wx_in) | copy-start | bytes 98308
  0.0 99.6 %copy-start.3 = (bf16[2,64,256]{2,1,0:T(8,128)(2,1)S(1)}, bf16[2,64,256]{2,1,0:T(8,128)(2,1)}, u32[]{:S(2)}) copy-start(bf16[2,64,256]{2,1,0:T(8,128)(2,1)} %constant.19.clone.vz_in) | copy-start | bytes 196612
  0.0 99.6 %copy-start.4 = (bf16[2,64,256]{2,1,0:T(8,128)(2,1)S(1)}, bf16[2,64,256]{2,1,0:T(8,128)(2,1)}, u32[]{:S(2)}) copy-start(bf16[2,64,256]{2,1,0:T(8,128)(2,1)} %constant.18.clone.vy_in) | copy-start | bytes 196612
  0.0 99.6 %copy-start = (bf16[1,16,128,256]{3,2,1,0:T(8,128)(2,1)S(1)}, bf16[1,16,128,256]{3,2,1,0:T(8,128)(2,1)}, u32[]{:S(2)}) copy-start(bf16[1,16,128,256]{3,2,1,0:T(8,128)(2,1)} %param.10) | copy-start | bytes 3145732
  0.0 99.6 %copy-start.8 = (f32[1,16]{1,0:T(1,128)S(1)}, f32[1,16]{1,0:T(1,128)}, u32[]{:S(2)}) copy-start(f32[1,16]{1,0:T(1,128)} %bias_ref.1) | copy-start | bytes 196
  0.0 99.6 %copy-start.7 = (f32[1,32,16]{1,2,0:T(8,128)S(1)}, f32[1,32,16]{1,2,0:T(8,128)}, u32[]{:S(2)}) copy-start(f32[1,32,16]{1,2,0:T(8,128)} %param.12) | copy-start | bytes 6148
  3.8 80.3 %all-to-all-start = ((f32[128,2,128]{2,1,0:T(2,128)}), f32[128,2,128]{2,1,0:T(2,128)S(1)}, u32[]{:S(2)}, u32[]{:S(2)}) async-start(f32[128,2,128]{2,1,0:T(2,128)} %bitcast.1), calls=%async_computation | async-start | bytes 262144 | tf_op jit(solution)/shard_map/all_to_all | solution.py:280
  57.0 41.7 %collective-permute-start = (bf16[16,128,256]{2,1,0:T(8,128)(2,1)}, bf16[16,128,256]{2,1,0:T(8,128)(2,1)S(1)}, u32[]{:S(2)}, u32[]{:S(2)}) collective-permute-start(bf16[16,128,256]{2,1,0:T(8,128)(2,1)} %bitcast.17), channel_id=1, source_target_pairs={{0,1},{1,0},{2,3},{3,2},{4,5},{5,4},{6,7},{7,6},{8,9},{9,8},{10,11... | collective-permute-start | bytes 3145736 | tf_op jit(solution)/shard_map/ppermute | solution.py:287
  87.2 38.4 %all-to-all-start.1 = ((f32[128,2,128]{2,1,0:T(2,128)}), f32[128,2,128]{2,1,0:T(2,128)S(1)}, u32[]{:S(2)}, u32[]{:S(2)}) async-start(f32[128,2,128]{2,1,0:T(2,128)} %bitcast.7), calls=%async_computation.1 | async-start | bytes 262144 | tf_op jit(solution)/shard_map/all_to_all | solution.py:280
  98.7 1.0 copy-start.1
  99.7 1.2 copy-start.2

commit v3 on v2

--- a/solution.py
+++ b/solution.py
@@ -23,6 +23,9 @@
 ORDER = [(place % PX) * PZ + place // PX for place in range(PX * PZ)]
 
 F32 = jnp.float32
+F16 = jnp.float16
+SCALE_MODES = 32.0
+SCALE_MIXED = 0.125
 BF16 = jnp.bfloat16
 
 
@@ -47,14 +50,14 @@
     cos_z, sin_z = tables(NZ, MZ)
     tz = np.concatenate(halves(np.concatenate([cos_z, -sin_z], 0) * NZ**-0.5), 0)
     wy = np.concatenate([np.concatenate([cos_y, sin_y], 1), np.concatenate([-sin_y, cos_y], 1)], 0)
-    wy = np.concatenate(halves(wy * NY**-0.5), 0)
+    wy = np.concatenate(halves(wy * (NY**-0.5 * SCALE_MODES)), 0)
     wx = np.concatenate([np.stack([cos_x, sin_x], 2), np.stack([-sin_x, cos_x], 2)], 0).reshape(2 * MX, 2 * NX)
-    wx = np.concatenate(halves(wx * NX**-0.5), 0)
+    wx = np.concatenate(halves(wx * (NX**-0.5 / SCALE_MODES)), 0)
     vx = np.stack([np.concatenate([cos_x, -sin_x], 0).T, np.concatenate([sin_x, cos_x], 0).T], 1)
-    high, low = halves(vx.reshape(2 * NX, 2 * MX) * MX**-0.5)
+    high, low = halves(vx.reshape(2 * NX, 2 * MX) * (MX**-0.5 * SCALE_MIXED))
     vx = np.concatenate([high, low, high], 1)
     vy = np.concatenate([np.concatenate([cos_y, sin_y], 1), np.concatenate([-sin_y, cos_y], 1)], 0)
-    vy = np.stack(halves(vy * MY**-0.5), 0)
+    vy = np.stack(halves(vy * (MY**-0.5 / SCALE_MIXED)), 0)
     vz = np.stack(halves(np.concatenate([cos_z, -sin_z], 0) * MZ**-0.5), 0)
     return tz, wy, wx, vx, vy, vz
 
@@ -277,8 +280,9 @@
 
 
 def exchange(value):
-    sent = lax.all_to_all(value.reshape(NX, 2, LC * K8), ("pz", "px"), 0, 0, tiled=True)
-    return sent.reshape(2 * NX, LC * K8)
+    sent = value.astype(F16).reshape(NX, 2, LC * K8)
+    sent = lax.all_to_all(sent, ("pz", "px"), 0, 0, tiled=True)
+    return sent.reshape(2 * NX, LC * K8).astype(F32)
 
 
 def local(features, spectral_weights, bypass_weights, bypass_bias):
@@ -302,6 +306,7 @@
 def solution(mesh):
     groups, _, cores = mesh.devices.shape
     chips = Mesh(mesh.devices.reshape(groups, PX, PZ, cores), ("grp", "px", "pz", "ch"))
+
     return jax.shard_map(
         local,
         mesh=chips,

time: 130 us -> 124 us (0.954)
  local copies, waits for them, and re-layouts: 3.82 us -> 1.64 us
  waiting for transfers between devices: 44.4 us -> 42.4 us
  other arithmetic: 0 us -> 1.31 us
  Pallas kernels: 12.3 us -> 11 us
    unnamed x18 -> x14, local copies, waits for them, and re-layouts: 2.22 us -> 0.03 us
    all_to_all x2, waiting for transfers between devices: 44.4 us -> 42.4 us  [exchange(): sent = lax.all_to_all(sent, ('pz', 'px'), 0, 0, tiled=True)]
    convert_element_type x0 -> x4, other arithmetic: none -> 1.31 us  [the longest x2 1.29 us: exchange(): sent = value.astype(F16).reshape(NX, 2, LC * K8)]
    all_to_all x2, starting transfers between devices: 64.6 us -> 63.3 us  [exchange(): sent = lax.all_to_all(sent, ('pz', 'px'), 0, 0, tiled=True)]
  transfers between devices with their start and end apart: 3 -> 3, of which waited for: 2 -> 2; matrix products, arithmetic and copies ran while one was open for 1% -> 2% of each run, Pallas kernels for 4% -> 0%
where the time goes in v3:
time: 124 us
  starting transfers between devices  65.3 us (53%)
  waiting for transfers between devices  42.4 us (34%)
  Pallas kernels  11 us (9%)
  blocking collectives  1.88 us (2%)
  local copies, waits for them, and re-layouts  1.64 us (1%)
  other arithmetic  1.31 us (1%)
    all_to_all x2, starting transfers between devices, exchange(): sent = lax.all_to_all(sent, ('pz', 'px'), 0, 0, tiled=True)  63.3 us
    all_to_all x2, waiting for transfers between devices, exchange(): sent = lax.all_to_all(sent, ('pz', 'px'), 0, 0, tiled=True)  42.4 us
    pallas_call x1, Pallas kernels, bypass_of(): pl.pallas_call(bypass_kernel, grid=(NY // BYPASS_ROWS,), in_specs=[smem,...  3.81 us
    pallas_call x1, Pallas kernels, inverse(): pl.pallas_call(inverse_kernel, grid=(INVERSE_STEPS,), in_specs=[VMEM] * 5...  3.54 us
    pallas_call x1, Pallas kernels, forward(): pl.pallas_call(forward_kernel, grid=(STEPS,), in_specs=[pl.BlockSpec((per...  3.08 us
  transfers between devices with their start and end apart: 3, of which 2 were waited for; matrix products, arithmetic and copies ran while one was open for 2% of the time, Pallas kernels for 0%

profile of v3, /device:TPU:40, one launch (start us, length us, event | category | flops | bytes accessed | tf_op | source)
XLA Modules:
  0.0 123.7 jit_solution(3138312319166183143)
XLA Ops:
  0.0 0.0 copy-start.3
  0.0 0.0 copy-start.4
  0.0 0.0 copy-start
  0.0 0.0 copy-start.1
  0.0 0.0 copy-start.2
  0.0 0.0 copy-start.5
  0.0 0.0 copy-start.6
  0.1 3.1 %forward.1 = f32[256,128]{1,0:T(8,128)S(1)} custom-call(bf16[16,128,256]{2,1,0:T(8,128)(2,1)} %bitcast.18, bf16[128,256]{1,0:T(8,128)(2,1)} %constant.16.clone.tz_ref, bf16[128,256]{1,0:T(8,128)(2,1)} %constant.17.clone.wy_ref), custom_call_target="tpu_custom_call" | custom-call | tf_op jit(solution)/shard_map/forward/pallas_call | solution.py:113
  3.1 0.6 convert_element_type.16
  3.8 53.2 %all-to-all-start = ((f16[128,2,128]{2,1,0:T(2,128)(2,1)}), f16[128,2,128]{2,1,0:T(2,128)(2,1)S(1)}, u32[]{:S(2)}, u32[]{:S(2)}) async-start(f16[128,2,128]{2,1,0:T(2,128)(2,1)} %bitcast.1), calls=%async_computation | async-start | bytes 131072 | tf_op jit(solution)/shard_map/all_to_all | solution.py:284
  57.0 2.0 %collective-permute-start = (bf16[16,128,256]{2,1,0:T(8,128)(2,1)}, bf16[16,128,256]{2,1,0:T(8,128)(2,1)S(1)}, u32[]{:S(2)}, u32[]{:S(2)}) collective-permute-start(bf16[16,128,256]{2,1,0:T(8,128)(2,1)} %bitcast.19), channel_id=1, source_target_pairs={{0,1},{1,0},{2,3},{3,2},{4,5},{5,4},{6,7},{7,6},{8,9},{9,8},{10,11... | collective-permute-start | bytes 3145736 | tf_op jit(solution)/shard_map/ppermute | solution.py:291
  58.9 1.6 %copy.12.w_ref = bf16[2,32,16,128]{3,2,1,0:T(8,128)(2,1)S(1)} copy(bf16[2,32,16,128]{1,3,2,0:T(8,128)(2,1)} %bitcast.24) | data formatting | bytes 524288 | tf_op jit(solution)/shard_map/reshape | solution.py:295
  60.5 0.0 copy-done.3
  60.5 0.0 copy-done.4
  60.6 19.2 %all-to-all-done = f16[128,2,128]{2,1,0:T(2,128)(2,1)S(1)} async-done(((f16[128,2,128]{2,1,0:T(2,128)(2,1)}), f16[128,2,128]{2,1,0:T(2,128)(2,1)S(1)}, u32[]{:S(2)}, u32[]{:S(2)}) %all-to-all-start) | async-done | bytes 65568 | tf_op jit(solution)/shard_map/all_to_all | solution.py:284
  79.8 0.1 x_forward.1
  80.0 1.9 %all-gather = f32[64,128]{1,0:T(8,128)S(1)} all-gather(f32[32,128]{1,0:T(8,128)S(1)} %x_forward.1), channel_id=2, replica_groups=mesh['grp'=2,'px'=4,'pz'=32,'ch'=2] {'ch'}, dimensions={0}, use_global_device_ids=true | all-gather | bytes 49152 | tf_op jit(solution)/shard_map/all_gather | solution.py:301
  81.8 0.4 mix.1
  82.3 0.6 convert_element_type.19
  83.0 10.1 %all-to-all-start.1 = ((f16[128,2,128]{2,1,0:T(2,128)(2,1)}), f16[128,2,128]{2,1,0:T(2,128)(2,1)S(1)}, u32[]{:S(2)}, u32[]{:S(2)}) async-start(f16[128,2,128]{2,1,0:T(2,128)(2,1)} %bitcast.7), calls=%async_computation.1 | async-start | bytes 131072 | tf_op jit(solution)/shard_map/all_to_all | solution.py:284
  93.1 23.1 %all-to-all-done.1 = f16[128,2,128]{2,1,0:T(2,128)(2,1)S(1)} async-done(((f16[128,2,128]{2,1,0:T(2,128)(2,1)}), f16[128,2,128]{2,1,0:T(2,128)(2,1)S(1)}, u32[]{:S(2)}, u32[]{:S(2)}) %all-to-all-start.1) | async-done | bytes 65568 | tf_op jit(solution)/shard_map/all_to_all | solution.py:284
  116.3 0.0 collective-permute-done.g_ref
  116.3 0.0 copy-done
  116.3 0.0 copy-done.1
  116.3 0.0 copy-done.2
  116.3 0.0 copy-done.5
  116.3 0.0 copy-done.6
  116.3 3.8 %bypass.1 = (f32[16,128,256]{2,1,0:T(8,128)S(1)}, bf16[2,64,256]{2,1,0:T(8,128)(2,1)S(1)}, bf16[2,64,256]{2,1,0:T(8,128)(2,1)S(1)}) custom-call(s32[1]{0:T(128)} %bitcast.9.core_ref, f32[1,16]{1,0:T(1,128)S(1)} %copy-done.6, f32[16,32]{1,0:T(8,128)S(1)} %bitcast.23, bf16[16,128,256]{2,1,0:T(8,128)(2,1)S(1)} %bitcast.20, ...), custom_call_target="tpu_custom_call" | custom-call | tf_op jit(solution)/shard_map/bypass/pallas_call | solution.py:215
  120.1 3.5 %inverse.1 = f32[16,128,256]{2,1,0:T(8,128)} custom-call(f32[256,128]{1,0:T(8,128)S(1)} %convert.3.h_ref, bf16[2,64,256]{2,1,0:T(8,128)(2,1)S(1)} %get-tuple-element.12.vy_ref, bf16[2,64,256]{2,1,0:T(8,128)(2,1)S(1)} %get-tuple-element.13.vz_ref, f32[16,128,256]{2,1,0:T(8,128)S(1)} %get-tuple-element.14.b_ref, bf16[16,128,256]{2,1,0:T(8,128)(2,1)S(1)} %bitcast.21), custom_call_target="tpu_custom_call" | custom-call | tf_op jit(solution)/shard_map/inverse/pallas_call | solution.py:270
  (3 shorter events, 0.0 us)
Async XLA Ops:
  0.0 60.5 %copy-start.3 = (bf16[256,96]{1,0:T(8,128)(2,1)S(1)}, bf16[256,96]{1,0:T(8,128)(2,1)}, u32[]{:S(2)}) copy-start(bf16[256,96]{1,0:T(8,128)(2,1)} %constant.21.clone.vx_in) | copy-start | bytes 147460
  0.0 60.5 %copy-start.4 = (bf16[64,256]{1,0:T(8,128)(2,1)S(1)}, bf16[64,256]{1,0:T(8,128)(2,1)}, u32[]{:S(2)}) copy-start(bf16[64,256]{1,0:T(8,128)(2,1)} %constant.20.clone.wx_in) | copy-start | bytes 98308
  0.0 116.3 %copy-start = (bf16[1,16,128,256]{3,2,1,0:T(8,128)(2,1)S(1)}, bf16[1,16,128,256]{3,2,1,0:T(8,128)(2,1)}, u32[]{:S(2)}) copy-start(bf16[1,16,128,256]{3,2,1,0:T(8,128)(2,1)} %param.10) | copy-start | bytes 3145732
  0.0 116.3 %copy-start.1 = (bf16[2,64,256]{2,1,0:T(8,128)(2,1)S(1)}, bf16[2,64,256]{2,1,0:T(8,128)(2,1)}, u32[]{:S(2)}) copy-start(bf16[2,64,256]{2,1,0:T(8,128)(2,1)} %constant.19.clone.vz_in) | copy-start | bytes 196612
  0.0 116.3 %copy-start.2 = (bf16[2,64,256]{2,1,0:T(8,128)(2,1)S(1)}, bf16[2,64,256]{2,1,0:T(8,128)(2,1)}, u32[]{:S(2)}) copy-start(bf16[2,64,256]{2,1,0:T(8,128)(2,1)} %constant.18.clone.vy_in) | copy-start | bytes 196612
  0.0 116.3 %copy-start.5 = (f32[1,32,16]{1,2,0:T(8,128)S(1)}, f32[1,32,16]{1,2,0:T(8,128)}, u32[]{:S(2)}) copy-start(f32[1,32,16]{1,2,0:T(8,128)} %param.12) | copy-start | bytes 6148
  0.0 116.3 %copy-start.6 = (f32[1,16]{1,0:T(1,128)S(1)}, f32[1,16]{1,0:T(1,128)}, u32[]{:S(2)}) copy-start(f32[1,16]{1,0:T(1,128)} %bias_ref.1) | copy-start | bytes 196
  3.8 76.0 %all-to-all-start = ((f16[128,2,128]{2,1,0:T(2,128)(2,1)}), f16[128,2,128]{2,1,0:T(2,128)(2,1)S(1)}, u32[]{:S(2)}, u32[]{:S(2)}) async-start(f16[128,2,128]{2,1,0:T(2,128)(2,1)} %bitcast.1), calls=%async_computation | async-start | bytes 131072 | tf_op jit(solution)/shard_map/all_to_all | solution.py:284
  57.0 59.3 %collective-permute-start = (bf16[16,128,256]{2,1,0:T(8,128)(2,1)}, bf16[16,128,256]{2,1,0:T(8,128)(2,1)S(1)}, u32[]{:S(2)}, u32[]{:S(2)}) collective-permute-start(bf16[16,128,256]{2,1,0:T(8,128)(2,1)} %bitcast.19), channel_id=1, source_target_pairs={{0,1},{1,0},{2,3},{3,2},{4,5},{5,4},{6,7},{7,6},{8,9},{9,8},{10,11... | collective-permute-start | bytes 3145736 | tf_op jit(solution)/shard_map/ppermute | solution.py:291
  83.0 33.3 %all-to-all-start.1 = ((f16[128,2,128]{2,1,0:T(2,128)(2,1)}), f16[128,2,128]{2,1,0:T(2,128)(2,1)S(1)}, u32[]{:S(2)}, u32[]{:S(2)}) async-start(f16[128,2,128]{2,1,0:T(2,128)(2,1)} %bitcast.7), calls=%async_computation.1 | async-start | bytes 131072 | tf_op jit(solution)/shard_map/all_to_all | solution.py:284

commit v4 on v3

--- a/solution.py
+++ b/solution.py
@@ -67,6 +67,10 @@
     return high, (value - high.astype(F32)).astype(BF16)
 
 
+def far(*values):
+    return tuple(pltpu.with_memory_space_constraint(jnp.asarray(v), pltpu.HBM) for v in values)
+
+
 def rows_of(b, n, part):
     return pl.ds(2 * PX * b + 2 * n + part, 8, stride=2 * PX * KB)
 
@@ -75,7 +79,7 @@
     return lax.dot_general(a, b, (dims, ((), ())), preferred_element_type=F32)
 
 
-STEPS = 4
+STEPS = 8
 VMEM = pl.BlockSpec(memory_space=pltpu.VMEM)
 PARAMS = pltpu.CompilerParams(vmem_limit_bytes=16 << 20)
 
@@ -123,7 +127,7 @@
         scratch_shapes=[pltpu.VMEM((KB, LC * K8, 2 * NY), F32)],
         name="forward",
         compiler_params=PARAMS,
-    )(*(pltpu.with_memory_space_constraint(v, pltpu.HBM) for v in (field, jnp.asarray(tz), jnp.asarray(wy))))
+    )(*far(field, tz, wy))
 
 
 def x_forward_kernel(s_ref, wx_ref, o_ref):
@@ -152,8 +156,7 @@
         at = within + (i % LC) * K8
         real = jnp.take_along_axis(x_ref[i // LC, :MX], at, axis=1)
         imag = jnp.take_along_axis(x_ref[i // LC, MX:], at, axis=1)
-        w_re = w_ref[0, i].astype(F32)
-        w_im = w_ref[1, i].astype(F32)
+        w_re, w_im = w_ref[0, i], w_ref[1, i]
         real_g += w_re * real - w_im * imag
         imag_g += w_re * imag + w_im * real
     high, low = split(jnp.concatenate([real_g, imag_g], 0))
@@ -174,7 +177,7 @@
 BYPASS_ROWS = 16
 
 
-def bypass_kernel(core_ref, bias_ref, w_ref, f_ref, g_ref, vy_in, vz_in, o_ref, vy_ref, vz_ref, w2_ref):
+def bypass_kernel(core_ref, bias_ref, w_ref, f_ref, g_ref, vy_in, vz_in, o_ref, field_ref, vy_ref, vz_ref, w2_ref):
     rows = LC * BYPASS_ROWS
     step = pl.program_id(0)
 
@@ -201,9 +204,10 @@
     at = pl.multiple_of(step * BYPASS_ROWS, BYPASS_ROWS)
     total = None
     for k, ref in enumerate((f_ref, g_ref)):
-        block = (ref[:, pl.ds(at, BYPASS_ROWS), :] if k == 0 else ref[...]).reshape(rows, NZ)
+        block = ref[...].reshape(rows, NZ)
         term = dot(w2_ref[k, 0], block) + dot(w2_ref[k, 1], block)
         total = term if total is None else total + term
+    field_ref[:, pl.ds(at, BYPASS_ROWS), :] = f_ref[...]
     for o in range(LC):
         o_ref[o, pl.ds(at, BYPASS_ROWS), :] = total[o * BYPASS_ROWS : (o + 1) * BYPASS_ROWS] + bias_ref[0, o]
 
@@ -212,35 +216,44 @@
     rows = LC * BYPASS_ROWS
     smem = pl.BlockSpec(memory_space=pltpu.SMEM)
     whole = pl.BlockSpec(weights.shape, lambda s: (0, 0))
+    block = pl.BlockSpec((LC, BYPASS_ROWS, NZ), lambda s: (0, s, 0))
     return pl.pallas_call(
         bypass_kernel,
         grid=(NY // BYPASS_ROWS,),
-        in_specs=[smem, smem, whole, VMEM, pl.BlockSpec((LC, BYPASS_ROWS, NZ), lambda s: (0, s, 0))]
+        in_specs=[smem, smem, whole, block, block]
         + [pl.BlockSpec(v.shape, lambda s: (0, 0, 0)) for v in (vy, vz)],
-        out_specs=[VMEM] * 3,
-        out_shape=[pltpu.VMEM((LC, NY, NZ), F32), pltpu.VMEM(vy.shape, BF16), pltpu.VMEM(vz.shape, BF16)],
+        out_specs=[VMEM] * 4,
+        out_shape=[pltpu.VMEM((LC, NY, NZ), F32), pltpu.VMEM((LC, NY, NZ), BF16), pltpu.VMEM(vy.shape, BF16), pltpu.VMEM(vz.shape, BF16)],
         scratch_shapes=[pltpu.VMEM((2, 2, rows, rows), BF16)],
         name="bypass",
         compiler_params=PARAMS,
-    )(core, bias, weights, *near(own), other, vy, vz)
-
-
-def stage_kernel(wx_in, vx_in, wx_ref, vx_ref):
+    )(core, bias, *far(weights, own, other, vy, vz))
+
+
+def stage_kernel(w_ref, wx_in, vx_in, o_ref, wx_ref, vx_ref):
     wx_ref[...] = wx_in[...]
     vx_ref[...] = vx_in[...]
-
-
-def stage(wx, vx):
+    for part in range(2):
+        for j in range(MX):
+            o_ref[part, :, j, :] = w_ref[part, j].astype(F32).T
+
+
+def stage(weights, wx, vx):
     return pl.pallas_call(
         stage_kernel,
-        out_specs=[VMEM] * 2,
-        out_shape=[pltpu.VMEM(wx.shape, BF16), pltpu.VMEM(vx.shape, BF16)],
+        out_specs=[VMEM] * 3,
+        out_shape=[
+            pltpu.VMEM((2, C, MX, LC * K8), F32),
+            pltpu.VMEM(wx.shape, BF16),
+            pltpu.VMEM(vx.shape, BF16),
+        ],
         name="stage",
         compiler_params=PARAMS,
-    )(wx, vx)
-
-
-INVERSE_STEPS = 4
+    )(*far(weights, wx, vx))
+
+
+GELU = float(np.sqrt(2.0 / np.pi))
+INVERSE_STEPS = 8
 
 
 def inverse_kernel(h_ref, vy_ref, vz_ref, b_ref, f_ref, o_ref, a_ref):
@@ -262,8 +275,9 @@
         ]
         high, low = split(jnp.concatenate(parts, 0).T)
         value = dot(high, vz_ref[0]) + dot(low, vz_ref[0]) + dot(high, vz_ref[1]) + b_ref[o]
-        gelu = 0.5 * value * (1.0 + jnp.tanh(np.sqrt(2.0 / np.pi) * (value + 0.044715 * value * value * value)))
-        o_ref[n] = f_ref[o].astype(F32) + gelu
+        half = 0.5 * value
+        bend = jnp.tanh(value * (GELU + (0.044715 * GELU) * (value * value)))
+        o_ref[n] = (f_ref[o].astype(F32) + half) + half * bend
 
 
 def inverse(sent, vy, vz, pre, field):
@@ -292,15 +306,14 @@
 
     modes = exchange(forward(field, tz, wy))
 
-    weights = spectral_weights[0].transpose(0, 2, 1, 3, 4).reshape(2, C, MX, LC * K8)
-
     core = lax.axis_index("ch").astype(jnp.int32)[None]
-    pre, vy, vz = bypass_of(core, bypass_bias, bypass_weights[0].T, field, other, vy, vz)
-
-    wx, vx = stage(wx, vx)
+    pre, near_field, vy, vz = bypass_of(core, bypass_bias, bypass_weights[0].T, field, other, vy, vz)
+
+    weights = spectral_weights[0].transpose(0, 1, 3, 4, 2).reshape(2, MX, LC * K8, C)
+    weights, wx, vx = stage(weights, wx, vx)
     both = lax.all_gather(x_forward(modes, wx), "ch")
     back = exchange(mix(both, weights, vx))
-    return inverse(back, vy, vz, pre, field)[None]
+    return inverse(back, vy, vz, pre, near_field)[None]
 
 
 def solution(mesh):

time: 124 us -> 131 us (1.056)
  Pallas kernels: 11 us -> 18.8 us
    pallas_call x1, Pallas kernels: 3.81 us -> 6.25 us  [bypass_of(): pl.pallas_call(bypass_kernel, grid=(NY // BYPASS_ROWS,), in_specs=[smem,...]
    pallas_call x1, Pallas kernels: 3.08 us -> 5.03 us  [forward(): pl.pallas_call(forward_kernel, grid=(STEPS,), in_specs=[pl.BlockSpec((per...]
    pallas_call x1, Pallas kernels: 0.02 us -> 1.73 us  [stage(): pl.pallas_call(stage_kernel, out_specs=[VMEM] * 3, out_shape=[pltpu.VMEM(...]
    pallas_call x1, Pallas kernels: 3.54 us -> 5.19 us  [inverse(): pl.pallas_call(inverse_kernel, grid=(INVERSE_STEPS,), in_specs=[VMEM] * 5...]
    reshape x1 -> x0, local copies, waits for them, and re-layouts: 1.61 us -> none  [local(): spectral_weights[0].transpose(0, 2, 1, 3, 4).reshape(2, C, MX, LC * K8)]
  transfers between devices with their start and end apart: 3 -> 3, of which waited for: 2 -> 2; matrix products, arithmetic and copies ran while one was open for 2% -> 1% of each run, Pallas kernels for 0% -> 2%
where the time goes in v4:
time: 131 us
  starting transfers between devices  65.3 us (50%)
  waiting for transfers between devices  42.3 us (32%)
  Pallas kernels  18.8 us (14%)
  blocking collectives  1.88 us (1%)
  other arithmetic  1.31 us (1%)
    all_to_all x2, starting transfers between devices, exchange(): sent = lax.all_to_all(sent, ('pz', 'px'), 0, 0, tiled=True)  63.3 us
    all_to_all x2, waiting for transfers between devices, exchange(): sent = lax.all_to_all(sent, ('pz', 'px'), 0, 0, tiled=True)  42.3 us
    pallas_call x1, Pallas kernels, bypass_of(): pl.pallas_call(bypass_kernel, grid=(NY // BYPASS_ROWS,), in_specs=[smem,...  6.25 us
    pallas_call x1, Pallas kernels, inverse(): pl.pallas_call(inverse_kernel, grid=(INVERSE_STEPS,), in_specs=[VMEM] * 5...  5.19 us
    pallas_call x1, Pallas kernels, forward(): pl.pallas_call(forward_kernel, grid=(STEPS,), in_specs=[pl.BlockSpec((per...  5.03 us
  transfers between devices with their start and end apart: 3, of which 2 were waited for; matrix products, arithmetic and copies ran while one was open for 1% of the time, Pallas kernels for 2%

profile of v4, /device:TPU:40, one launch (start us, length us, event | category | flops | bytes accessed | tf_op | source)
XLA Modules:
  0.0 130.6 jit_solution(15481309346249249731)
XLA Ops:
  0.0 0.0 copy-start
  0.0 5.0 %forward.1 = f32[256,128]{1,0:T(8,128)S(1)} custom-call(bf16[16,128,256]{2,1,0:T(8,128)(2,1)} %bitcast.19, bf16[128,256]{1,0:T(8,128)(2,1)} %constant.16.clone.tz_ref, bf16[128,256]{1,0:T(8,128)(2,1)} %constant.17.clone.wy_ref), custom_call_target="tpu_custom_call" | custom-call | tf_op jit(solution)/shard_map/forward/pallas_call | solution.py:117
  5.0 0.6 convert_element_type.16
  5.7 53.2 %all-to-all-start = ((f16[128,2,128]{2,1,0:T(2,128)(2,1)}), f16[128,2,128]{2,1,0:T(2,128)(2,1)S(1)}, u32[]{:S(2)}, u32[]{:S(2)}) async-start(f16[128,2,128]{2,1,0:T(2,128)(2,1)} %bitcast.1), calls=%async_computation | async-start | bytes 131072 | tf_op jit(solution)/shard_map/all_to_all | solution.py:298
  58.9 2.0 %collective-permute-start = (bf16[16,128,256]{2,1,0:T(8,128)(2,1)}, bf16[16,128,256]{2,1,0:T(8,128)(2,1)S(1)}, u32[]{:S(2)}, u32[]{:S(2)}) collective-permute-start(bf16[16,128,256]{2,1,0:T(8,128)(2,1)} %bitcast.20), channel_id=1, source_target_pairs={{0,1},{1,0},{2,3},{3,2},{4,5},{5,4},{6,7},{7,6},{8,9},{9,8},{10,11... | collective-permute-start | bytes 3145736 | tf_op jit(solution)/shard_map/ppermute | solution.py:305
  60.8 1.7 %stage.1 = (f32[2,32,16,128]{3,2,1,0:T(8,128)S(1)}, bf16[64,256]{1,0:T(8,128)(2,1)S(1)}, bf16[256,96]{1,0:T(8,128)(2,1)S(1)}) custom-call(bf16[2,16,128,32]{3,2,1,0:T(8,128)(2,1)} %bitcast.22, bf16[64,256]{1,0:T(8,128)(2,1)} %constant.20.clone.wx_in, bf16[256,96]{1,0:T(8,128)(2,1)} %constant.21.clone.vx_in), custom_call_target="tpu_custom_call" | custom-call | tf_op jit(solution)/shard_map/stage/pallas_call | solution.py:242
  62.6 19.1 %all-to-all-done = f16[128,2,128]{2,1,0:T(2,128)(2,1)S(1)} async-done(((f16[128,2,128]{2,1,0:T(2,128)(2,1)}), f16[128,2,128]{2,1,0:T(2,128)(2,1)S(1)}, u32[]{:S(2)}, u32[]{:S(2)}) %all-to-all-start) | async-done | bytes 65568 | tf_op jit(solution)/shard_map/all_to_all | solution.py:298
  81.7 0.1 x_forward.1
  81.9 1.9 %all-gather = f32[64,128]{1,0:T(8,128)S(1)} all-gather(f32[32,128]{1,0:T(8,128)S(1)} %x_forward.1), channel_id=2, replica_groups=mesh['grp'=2,'px'=4,'pz'=32,'ch'=2] {'ch'}, dimensions={0}, use_global_device_ids=true | all-gather | bytes 49152 | tf_op jit(solution)/shard_map/all_gather | solution.py:314
  83.7 0.4 mix.1
  84.2 0.7 convert_element_type.19
  84.8 10.1 %all-to-all-start.1 = ((f16[128,2,128]{2,1,0:T(2,128)(2,1)}), f16[128,2,128]{2,1,0:T(2,128)(2,1)S(1)}, u32[]{:S(2)}, u32[]{:S(2)}) async-start(f16[128,2,128]{2,1,0:T(2,128)(2,1)} %bitcast.7), calls=%async_computation.1 | async-start | bytes 131072 | tf_op jit(solution)/shard_map/all_to_all | solution.py:298
  95.0 23.1 %all-to-all-done.1 = f16[128,2,128]{2,1,0:T(2,128)(2,1)S(1)} async-done(((f16[128,2,128]{2,1,0:T(2,128)(2,1)}), f16[128,2,128]{2,1,0:T(2,128)(2,1)S(1)}, u32[]{:S(2)}, u32[]{:S(2)}) %all-to-all-start.1) | async-done | bytes 65568 | tf_op jit(solution)/shard_map/all_to_all | solution.py:298
  118.1 0.0 collective-permute-done.g_ref
  118.1 0.0 copy-start.1
  118.2 1.0 copy-done.1
  119.1 0.0 copy-done
  119.1 6.3 %bypass.1 = (f32[16,128,256]{2,1,0:T(8,128)S(1)}, bf16[16,128,256]{2,1,0:T(8,128)(2,1)S(1)}, bf16[2,64,256]{2,1,0:T(8,128)(2,1)S(1)}, bf16[2,64,256]{2,1,0:T(8,128)(2,1)S(1)}) custom-call(s32[1]{0:T(128)} %bitcast.9.core_ref, f32[1,16]{1,0:T(1,128)S(1)} %copy-done, f32[16,32]{1,0:T(8,128)} %bitcast.25, bf16[16,128,256]{2,1,0:T(8,128)(2,1)} %bitcast.21, ...), custom_call_target="tpu_custom_call" | custom-call | tf_op jit(solution)/shard_map/bypass/pallas_call | solution.py:220
  125.4 5.2 %inverse.1 = f32[16,128,256]{2,1,0:T(8,128)} custom-call(f32[256,128]{1,0:T(8,128)S(1)} %convert.3.h_ref, bf16[2,64,256]{2,1,0:T(8,128)(2,1)S(1)} %get-tuple-element.15.vy_ref, bf16[2,64,256]{2,1,0:T(8,128)(2,1)S(1)} %get-tuple-element.16.vz_ref, f32[16,128,256]{2,1,0:T(8,128)S(1)} %get-tuple-element.17.b_ref, bf16[16,128,256]{2,1,0:T(8,128)(2,1)S(1)} %get-tuple-element.18.f_ref), custom_call_target="tpu_custom_call" | custom-call | tf_op jit(solution)/shard_map/inverse/pallas_call | solution.py:284
  (2 shorter events, 0.0 us)
Async XLA Ops:
  0.0 119.1 %copy-start = (f32[1,16]{1,0:T(1,128)S(1)}, f32[1,16]{1,0:T(1,128)}, u32[]{:S(2)}) copy-start(f32[1,16]{1,0:T(1,128)} %bias_ref.1) | copy-start | bytes 196
  5.7 76.0 %all-to-all-start = ((f16[128,2,128]{2,1,0:T(2,128)(2,1)}), f16[128,2,128]{2,1,0:T(2,128)(2,1)S(1)}, u32[]{:S(2)}, u32[]{:S(2)}) async-start(f16[128,2,128]{2,1,0:T(2,128)(2,1)} %bitcast.1), calls=%async_computation | async-start | bytes 131072 | tf_op jit(solution)/shard_map/all_to_all | solution.py:298
  58.9 59.3 %collective-permute-start = (bf16[16,128,256]{2,1,0:T(8,128)(2,1)}, bf16[16,128,256]{2,1,0:T(8,128)(2,1)S(1)}, u32[]{:S(2)}, u32[]{:S(2)}) collective-permute-start(bf16[16,128,256]{2,1,0:T(8,128)(2,1)} %bitcast.20), channel_id=1, source_target_pairs={{0,1},{1,0},{2,3},{3,2},{4,5},{5,4},{6,7},{7,6},{8,9},{9,8},{10,11... | collective-permute-start | bytes 3145736 | tf_op jit(solution)/shard_map/ppermute | solution.py:305
  84.8 33.3 %all-to-all-start.1 = ((f16[128,2,128]{2,1,0:T(2,128)(2,1)}), f16[128,2,128]{2,1,0:T(2,128)(2,1)S(1)}, u32[]{:S(2)}, u32[]{:S(2)}) async-start(f16[128,2,128]{2,1,0:T(2,128)(2,1)} %bitcast.7), calls=%async_computation.1 | async-start | bytes 131072 | tf_op jit(solution)/shard_map/all_to_all | solution.py:298
  118.1 1.0 copy-start.1

commit v5 on v4

--- a/solution.py
+++ b/solution.py
@@ -58,7 +58,8 @@
     vx = np.concatenate([high, low, high], 1)
     vy = np.concatenate([np.concatenate([cos_y, sin_y], 1), np.concatenate([-sin_y, cos_y], 1)], 0)
     vy = np.stack(halves(vy * (MY**-0.5 / SCALE_MIXED)), 0)
-    vz = np.stack(halves(np.concatenate([cos_z, -sin_z], 0) * MZ**-0.5), 0)
+    high, low = halves(np.concatenate([cos_z, -sin_z], 0) * (0.5 * MZ**-0.5))
+    vz = np.concatenate([high, high, low], 0)
     return tz, wy, wx, vx, vy, vz
 
 
@@ -79,7 +80,7 @@
     return lax.dot_general(a, b, (dims, ((), ())), preferred_element_type=F32)
 
 
-STEPS = 8
+STEPS = 4
 VMEM = pl.BlockSpec(memory_space=pltpu.VMEM)
 PARAMS = pltpu.CompilerParams(vmem_limit_bytes=16 << 20)
 
@@ -88,43 +89,55 @@
     return tuple(pltpu.with_memory_space_constraint(v, pltpu.VMEM) for v in values)
 
 
-def forward_kernel(f_ref, tz_ref, wy_ref, o_ref, z_ref):
-    step = pl.program_id(0)
+def forward_kernel(f_hbm, tz_hbm, wy_hbm, o_ref, f_ref, tz_ref, wy_ref, z_ref, sems):
     per = LC // STEPS
-    for n in range(per):
-        rows = dot(tz_ref[...], f_ref[n], ((1,), (1,)))
-        rows = rows[: 2 * MZ] + rows[2 * MZ :]
-        at = pl.multiple_of((step * per + n) * K8, K8)
-        for part in range(2):
-            for b in range(KB):
-                lo = part * MZ + b * K8
-                z_ref[b, pl.ds(at, K8), part * NY : (part + 1) * NY] = rows[lo : lo + K8]
-
-    @pl.when(step == STEPS - 1)
-    def _():
-        for b in range(KB):
-            high, low = split(z_ref[b])
-            out = dot(wy_ref[...], high, ((1,), (1,)))
-            out = out[: 2 * MY] + out[2 * MY :] + dot(wy_ref[: 2 * MY], low, ((1,), (1,)))
+    tz_copy = pltpu.make_async_copy(tz_hbm, tz_ref, sems.at[0])
+    wy_copy = pltpu.make_async_copy(wy_hbm, wy_ref, sems.at[1])
+    chunks = [
+        pltpu.make_async_copy(f_hbm.at[pl.ds(n * per, per)], f_ref.at[pl.ds(n * per, per)], sems.at[2 + n])
+        for n in range(STEPS)
+    ]
+    tz_copy.start()
+    for copy in chunks:
+        copy.start()
+    wy_copy.start()
+    tz_copy.wait()
+    for n, copy in enumerate(chunks):
+        copy.wait()
+        for first in range(n * per, (n + 1) * per, 2):
+            rows = dot(tz_ref[...], f_ref[first : first + 2].reshape(2 * NY, NZ), ((1,), (1,)))
+            rows = rows[: 2 * MZ] + rows[2 * MZ :]
+            for i in range(2):
+                at = (first + i) * K8
+                for part in range(2):
+                    for b in range(KB):
+                        lo = part * MZ + b * K8
+                        z_ref[b, at : at + K8, part * NY : (part + 1) * NY] = rows[lo : lo + K8, i * NY : (i + 1) * NY]
+    wy_copy.wait()
+    for pair in range(KB // 2):
+        high, low = split(z_ref[2 * pair : 2 * pair + 2].reshape(2 * LC * K8, 2 * NY))
+        out = dot(wy_ref[...], high, ((1,), (1,)))
+        out = out[: 2 * MY] + out[2 * MY :] + dot(wy_ref[: 2 * MY], low, ((1,), (1,)))
+        for i in range(2):
             for part in range(2):
                 for n in range(PX):
                     lo = part * MY + n * 8
-                    o_ref[rows_of(b, n, part), :] = out[lo : lo + 8]
+                    o_ref[rows_of(2 * pair + i, n, part), :] = out[lo : lo + 8, i * LC * K8 : (i + 1) * LC * K8]
 
 
 def forward(field, tz, wy):
-    per = LC // STEPS
     return pl.pallas_call(
         forward_kernel,
-        grid=(STEPS,),
-        in_specs=[
-            pl.BlockSpec((per, NY, NZ), lambda s: (s, 0, 0)),
-            pl.BlockSpec(tz.shape, lambda s: (0, 0)),
-            pl.BlockSpec(wy.shape, lambda s: (0, 0)),
-        ],
+        in_specs=[pl.BlockSpec(memory_space=pl.ANY)] * 3,
         out_specs=VMEM,
         out_shape=pltpu.VMEM((2 * MY * KB, LC * K8), F32),
-        scratch_shapes=[pltpu.VMEM((KB, LC * K8, 2 * NY), F32)],
+        scratch_shapes=[
+            pltpu.VMEM(field.shape, BF16),
+            pltpu.VMEM(tz.shape, BF16),
+            pltpu.VMEM(wy.shape, BF16),
+            pltpu.VMEM((KB, LC * K8, 2 * NY), F32),
+            pltpu.SemaphoreType.DMA((2 + STEPS,)),
+        ],
         name="forward",
         compiler_params=PARAMS,
     )(*far(field, tz, wy))
@@ -192,7 +205,7 @@
         col_of = lax.broadcasted_iota(jnp.int32, (C, rows), 1) // BYPASS_ROWS
         channel = lax.broadcasted_iota(jnp.int32, (C, rows), 0)
         core = core_ref[0]
-        for n, part in enumerate(split(w_ref[...])):
+        for n, part in enumerate(split(0.5 * w_ref[...])):
             tall = dot(left, part).astype(BF16)
             for k in range(2):
                 first = LC * (core if k == 0 else 1 - core)
@@ -209,7 +222,7 @@
         total = term if total is None else total + term
     field_ref[:, pl.ds(at, BYPASS_ROWS), :] = f_ref[...]
     for o in range(LC):
-        o_ref[o, pl.ds(at, BYPASS_ROWS), :] = total[o * BYPASS_ROWS : (o + 1) * BYPASS_ROWS] + bias_ref[0, o]
+        o_ref[o, pl.ds(at, BYPASS_ROWS), :] = total[o * BYPASS_ROWS : (o + 1) * BYPASS_ROWS] + 0.5 * bias_ref[0, o]
 
 
 def bypass_of(core, bias, weights, own, other, vy, vz):
@@ -221,7 +234,7 @@
         bypass_kernel,
         grid=(NY // BYPASS_ROWS,),
         in_specs=[smem, smem, whole, block, block]
-        + [pl.BlockSpec(v.shape, lambda s: (0, 0, 0)) for v in (vy, vz)],
+        + [pl.BlockSpec(v.shape, lambda s, n=v.ndim: (0,) * n) for v in (vy, vz)],
         out_specs=[VMEM] * 4,
         out_shape=[pltpu.VMEM((LC, NY, NZ), F32), pltpu.VMEM((LC, NY, NZ), BF16), pltpu.VMEM(vy.shape, BF16), pltpu.VMEM(vz.shape, BF16)],
         scratch_shapes=[pltpu.VMEM((2, 2, rows, rows), BF16)],
@@ -253,41 +266,46 @@
 
 
 GELU = float(np.sqrt(2.0 / np.pi))
-INVERSE_STEPS = 8
-
-
-def inverse_kernel(h_ref, vy_ref, vz_ref, b_ref, f_ref, o_ref, a_ref):
-    step = pl.program_id(0)
-    per = LC // INVERSE_STEPS
-
-    @pl.when(step == 0)
-    def _():
-        for b in range(KB):
-            parts = [h_ref[rows_of(b, n, part), :] for part in range(2) for n in range(PX)]
-            high, low = split(jnp.concatenate(parts, 0).T)
-            a_ref[b] = dot(high, vy_ref[0]) + dot(low, vy_ref[0]) + dot(high, vy_ref[1])
-
-    for n in range(per):
-        o = step * per + n
-        at = pl.multiple_of(o * K8, K8)
+TOGETHER = 2
+
+
+def inverse_kernel(h_ref, vy_ref, vz_ref, b_ref, f_ref, o_hbm, a_ref, out_ref, sems):
+    sides = []
+    for b in range(KB):
+        sides.append(jnp.concatenate([h_ref[rows_of(b, n, part), :] for part in range(2) for n in range(PX)], 0).T)
+    high, low = split(jnp.concatenate(sides, 0))
+    a_ref[...] = dot(high, vy_ref[0]) + dot(low, vy_ref[0]) + dot(high, vy_ref[1])
+
+    copies = []
+    for o in range(LC):
         parts = [
-            a_ref[b, pl.ds(at, K8), part * NY : (part + 1) * NY] for part in range(2) for b in range(KB)
+            a_ref[b * LC * K8 + o * K8 : b * LC * K8 + (o + 1) * K8, part * NY : (part + 1) * NY]
+            for part in range(2)
+            for b in range(KB)
         ]
-        high, low = split(jnp.concatenate(parts, 0).T)
-        value = dot(high, vz_ref[0]) + dot(low, vz_ref[0]) + dot(high, vz_ref[1]) + b_ref[o]
-        half = 0.5 * value
-        bend = jnp.tanh(value * (GELU + (0.044715 * GELU) * (value * value)))
-        o_ref[n] = (f_ref[o].astype(F32) + half) + half * bend
+        high, low = split(jnp.concatenate(parts, 0))
+        half = dot(jnp.concatenate([high, low, high], 0).T, vz_ref[...]) + b_ref[o]
+        bend = jnp.tanh(half * (2.0 * GELU + (8.0 * 0.044715 * GELU) * (half * half)))
+        out_ref[o] = (f_ref[o].astype(F32) + half) + half * bend
+        if (o + 1) % TOGETHER == 0:
+            rows = pl.ds(o + 1 - TOGETHER, TOGETHER)
+            copies.append(pltpu.make_async_copy(out_ref.at[rows], o_hbm.at[rows], sems.at[o // TOGETHER]))
+            copies[-1].start()
+    for copy in copies:
+        copy.wait()
 
 
 def inverse(sent, vy, vz, pre, field):
     return pl.pallas_call(
         inverse_kernel,
-        grid=(INVERSE_STEPS,),
         in_specs=[VMEM] * 5,
-        out_specs=pl.BlockSpec((LC // INVERSE_STEPS, NY, NZ), lambda s: (s, 0, 0)),
+        out_specs=pl.BlockSpec(memory_space=pl.ANY),
         out_shape=jax.ShapeDtypeStruct((LC, NY, NZ), F32),
-        scratch_shapes=[pltpu.VMEM((KB, LC * K8, 2 * NY), F32)],
+        scratch_shapes=[
+            pltpu.VMEM((KB * LC * K8, 2 * NY), F32),
+            pltpu.VMEM((LC, NY, NZ), F32),
+            pltpu.SemaphoreType.DMA((LC // TOGETHER,)),
+        ],
         name="inverse",
         compiler_params=PARAMS,
     )(*near(sent, vy, vz, pre, field))

time: 131 us -> 125 us (0.954)
  Pallas kernels: 18.8 us -> 13.3 us
    pallas_call x2, Pallas kernels: 10.2 us -> 4.63 us  [the longest x1 2.34 us: inverse(): pl.pallas_call(inverse_kernel, in_specs=[VMEM] * 5, out_specs=pl.BlockSpe...]
where the time goes in v5:
time: 125 us
  starting transfers between devices  65.3 us (52%)
  waiting for transfers between devices  42.3 us (34%)
  Pallas kernels  13.3 us (11%)
  blocking collectives  1.88 us (2%)
  other arithmetic  1.31 us (1%)
    all_to_all x2, starting transfers between devices, exchange(): sent = lax.all_to_all(sent, ('pz', 'px'), 0, 0, tiled=True)  63.3 us
    all_to_all x2, waiting for transfers between devices, exchange(): sent = lax.all_to_all(sent, ('pz', 'px'), 0, 0, tiled=True)  42.3 us
    pallas_call x1, Pallas kernels, bypass_of(): pl.pallas_call(bypass_kernel, grid=(NY // BYPASS_ROWS,), in_specs=[smem,...  6.31 us
  transfers between devices with their start and end apart: 3, of which 2 were waited for; matrix products, arithmetic and copies ran while one was open for 1% of the time, Pallas kernels for 2%

profile of v5, /device:TPU:40, one launch (start us, length us, event | category | flops | bytes accessed | tf_op | source)
XLA Modules:
  0.0 125.1 jit_solution(6002533641253067287)
XLA Ops:
  0.0 0.0 copy-start
  0.0 2.3 %forward.1 = f32[256,128]{1,0:T(8,128)S(1)} custom-call(bf16[16,128,256]{2,1,0:T(8,128)(2,1)} %bitcast.19, bf16[128,256]{1,0:T(8,128)(2,1)} %constant.16.clone.tz_hbm, bf16[128,256]{1,0:T(8,128)(2,1)} %constant.17.clone.wy_hbm), custom_call_target="tpu_custom_call" | custom-call | tf_op jit(solution)/shard_map/forward/pallas_call | solution.py:129
  2.3 0.6 convert_element_type.16
  2.9 53.2 %all-to-all-start = ((f16[128,2,128]{2,1,0:T(2,128)(2,1)}), f16[128,2,128]{2,1,0:T(2,128)(2,1)S(1)}, u32[]{:S(2)}, u32[]{:S(2)}) async-start(f16[128,2,128]{2,1,0:T(2,128)(2,1)} %bitcast.1), calls=%async_computation | async-start | bytes 131072 | tf_op jit(solution)/shard_map/all_to_all | solution.py:316
  56.1 2.0 %collective-permute-start = (bf16[16,128,256]{2,1,0:T(8,128)(2,1)}, bf16[16,128,256]{2,1,0:T(8,128)(2,1)S(1)}, u32[]{:S(2)}, u32[]{:S(2)}) collective-permute-start(bf16[16,128,256]{2,1,0:T(8,128)(2,1)} %bitcast.20), channel_id=1, source_target_pairs={{0,1},{1,0},{2,3},{3,2},{4,5},{5,4},{6,7},{7,6},{8,9},{9,8},{10,11... | collective-permute-start | bytes 3145736 | tf_op jit(solution)/shard_map/ppermute | solution.py:323
  58.1 1.7 %stage.1 = (f32[2,32,16,128]{3,2,1,0:T(8,128)S(1)}, bf16[64,256]{1,0:T(8,128)(2,1)S(1)}, bf16[256,96]{1,0:T(8,128)(2,1)S(1)}) custom-call(bf16[2,16,128,32]{3,2,1,0:T(8,128)(2,1)} %bitcast.22, bf16[64,256]{1,0:T(8,128)(2,1)} %constant.20.clone.wx_in, bf16[256,96]{1,0:T(8,128)(2,1)} %constant.21.clone.vx_in), custom_call_target="tpu_custom_call" | custom-call | tf_op jit(solution)/shard_map/stage/pallas_call | solution.py:255
  59.8 19.1 %all-to-all-done = f16[128,2,128]{2,1,0:T(2,128)(2,1)S(1)} async-done(((f16[128,2,128]{2,1,0:T(2,128)(2,1)}), f16[128,2,128]{2,1,0:T(2,128)(2,1)S(1)}, u32[]{:S(2)}, u32[]{:S(2)}) %all-to-all-start) | async-done | bytes 65568 | tf_op jit(solution)/shard_map/all_to_all | solution.py:316
  79.0 0.1 x_forward.1
  79.1 1.9 %all-gather = f32[64,128]{1,0:T(8,128)S(1)} all-gather(f32[32,128]{1,0:T(8,128)S(1)} %x_forward.1), channel_id=2, replica_groups=mesh['grp'=2,'px'=4,'pz'=32,'ch'=2] {'ch'}, dimensions={0}, use_global_device_ids=true | all-gather | bytes 49152 | tf_op jit(solution)/shard_map/all_gather | solution.py:332
  81.0 0.4 mix.1
  81.4 0.6 convert_element_type.19
  82.1 10.1 %all-to-all-start.1 = ((f16[128,2,128]{2,1,0:T(2,128)(2,1)}), f16[128,2,128]{2,1,0:T(2,128)(2,1)S(1)}, u32[]{:S(2)}, u32[]{:S(2)}) async-start(f16[128,2,128]{2,1,0:T(2,128)(2,1)} %bitcast.7), calls=%async_computation.1 | async-start | bytes 131072 | tf_op jit(solution)/shard_map/all_to_all | solution.py:316
  92.2 23.2 %all-to-all-done.1 = f16[128,2,128]{2,1,0:T(2,128)(2,1)S(1)} async-done(((f16[128,2,128]{2,1,0:T(2,128)(2,1)}), f16[128,2,128]{2,1,0:T(2,128)(2,1)S(1)}, u32[]{:S(2)}, u32[]{:S(2)}) %all-to-all-start.1) | async-done | bytes 65568 | tf_op jit(solution)/shard_map/all_to_all | solution.py:316
  115.5 0.0 collective-permute-done.g_ref
  115.5 0.0 copy-start.1
  115.5 1.0 copy-done.1
  116.5 0.0 copy-done
  116.5 6.3 %bypass.1 = (f32[16,128,256]{2,1,0:T(8,128)S(1)}, bf16[16,128,256]{2,1,0:T(8,128)(2,1)S(1)}, bf16[2,64,256]{2,1,0:T(8,128)(2,1)S(1)}, bf16[192,256]{1,0:T(8,128)(2,1)S(1)}) custom-call(s32[1]{0:T(128)} %bitcast.9.core_ref, f32[1,16]{1,0:T(1,128)S(1)} %copy-done, f32[16,32]{1,0:T(8,128)} %bitcast.25, bf16[16,128,256]{2,1,0:T(8,128)(2,1)} %bitcast.21, ...), custom_call_target="tpu_custom_call" | custom-call | tf_op jit(solution)/shard_map/bypass/pallas_call | solution.py:233
  122.8 2.3 %inverse.1 = f32[16,128,256]{2,1,0:T(8,128)} custom-call(f32[256,128]{1,0:T(8,128)S(1)} %convert.3.h_ref, bf16[2,64,256]{2,1,0:T(8,128)(2,1)S(1)} %get-tuple-element.15.vy_ref, bf16[192,256]{1,0:T(8,128)(2,1)S(1)} %get-tuple-element.16.vz_ref, f32[16,128,256]{2,1,0:T(8,128)S(1)} %get-tuple-element.17.b_ref, bf16[16,128,256]{2,1,0:T(8,128)(2,1)S(1)} %get-tuple-element.18.f_ref), custom_call_target="tpu_custom_call" | custom-call | tf_op jit(solution)/shard_map/inverse/pallas_call | solution.py:299
  (2 shorter events, 0.0 us)
Async XLA Ops:
  0.0 116.5 %copy-start = (f32[1,16]{1,0:T(1,128)S(1)}, f32[1,16]{1,0:T(1,128)}, u32[]{:S(2)}) copy-start(f32[1,16]{1,0:T(1,128)} %bias_ref.1) | copy-start | bytes 196
  2.9 76.0 %all-to-all-start = ((f16[128,2,128]{2,1,0:T(2,128)(2,1)}), f16[128,2,128]{2,1,0:T(2,128)(2,1)S(1)}, u32[]{:S(2)}, u32[]{:S(2)}) async-start(f16[128,2,128]{2,1,0:T(2,128)(2,1)} %bitcast.1), calls=%async_computation | async-start | bytes 131072 | tf_op jit(solution)/shard_map/all_to_all | solution.py:316
  56.1 59.3 %collective-permute-start = (bf16[16,128,256]{2,1,0:T(8,128)(2,1)}, bf16[16,128,256]{2,1,0:T(8,128)(2,1)S(1)}, u32[]{:S(2)}, u32[]{:S(2)}) collective-permute-start(bf16[16,128,256]{2,1,0:T(8,128)(2,1)} %bitcast.20), channel_id=1, source_target_pairs={{0,1},{1,0},{2,3},{3,2},{4,5},{5,4},{6,7},{7,6},{8,9},{9,8},{10,11... | collective-permute-start | bytes 3145736 | tf_op jit(solution)/shard_map/ppermute | solution.py:323
  82.1 33.4 %all-to-all-start.1 = ((f16[128,2,128]{2,1,0:T(2,128)(2,1)}), f16[128,2,128]{2,1,0:T(2,128)(2,1)S(1)}, u32[]{:S(2)}, u32[]{:S(2)}) async-start(f16[128,2,128]{2,1,0:T(2,128)(2,1)} %bitcast.7), calls=%async_computation.1 | async-start | bytes 131072 | tf_op jit(solution)/shard_map/all_to_all | solution.py:316
  115.5 1.0 copy-start.1

commit v6 on v5

--- a/solution.py
+++ b/solution.py
@@ -93,17 +93,15 @@
     per = LC // STEPS
     tz_copy = pltpu.make_async_copy(tz_hbm, tz_ref, sems.at[0])
     wy_copy = pltpu.make_async_copy(wy_hbm, wy_ref, sems.at[1])
-    chunks = [
-        pltpu.make_async_copy(f_hbm.at[pl.ds(n * per, per)], f_ref.at[pl.ds(n * per, per)], sems.at[2 + n])
-        for n in range(STEPS)
-    ]
+    copies = [pltpu.make_async_copy(f_hbm.at[i], f_ref.at[i], sems.at[2 + i]) for i in range(LC)]
     tz_copy.start()
-    for copy in chunks:
+    for copy in copies:
         copy.start()
     wy_copy.start()
     tz_copy.wait()
-    for n, copy in enumerate(chunks):
-        copy.wait()
+    for n in range(STEPS):
+        for copy in copies[n * per : (n + 1) * per]:
+            copy.wait()
         for first in range(n * per, (n + 1) * per, 2):
             rows = dot(tz_ref[...], f_ref[first : first + 2].reshape(2 * NY, NZ), ((1,), (1,)))
             rows = rows[: 2 * MZ] + rows[2 * MZ :]
@@ -136,7 +134,7 @@
             pltpu.VMEM(tz.shape, BF16),
             pltpu.VMEM(wy.shape, BF16),
             pltpu.VMEM((KB, LC * K8, 2 * NY), F32),
-            pltpu.SemaphoreType.DMA((2 + STEPS,)),
+            pltpu.SemaphoreType.DMA((2 + LC,)),
         ],
         name="forward",
         compiler_params=PARAMS,
@@ -190,7 +188,7 @@
 BYPASS_ROWS = 16
 
 
-def bypass_kernel(core_ref, bias_ref, w_ref, f_ref, g_ref, vy_in, vz_in, o_ref, field_ref, vy_ref, vz_ref, w2_ref):
+def bypass_kernel(core_ref, bias_ref, w_ref, f_ref, g_ref, vy_in, vz_in, o_ref, vy_ref, vz_ref, w2_ref):
     rows = LC * BYPASS_ROWS
     step = pl.program_id(0)
 
@@ -220,7 +218,6 @@
         block = ref[...].reshape(rows, NZ)
         term = dot(w2_ref[k, 0], block) + dot(w2_ref[k, 1], block)
         total = term if total is None else total + term
-    field_ref[:, pl.ds(at, BYPASS_ROWS), :] = f_ref[...]
     for o in range(LC):
         o_ref[o, pl.ds(at, BYPASS_ROWS), :] = total[o * BYPASS_ROWS : (o + 1) * BYPASS_ROWS] + 0.5 * bias_ref[0, o]
 
@@ -235,8 +232,8 @@
         grid=(NY // BYPASS_ROWS,),
         in_specs=[smem, smem, whole, block, block]
         + [pl.BlockSpec(v.shape, lambda s, n=v.ndim: (0,) * n) for v in (vy, vz)],
-        out_specs=[VMEM] * 4,
-        out_shape=[pltpu.VMEM((LC, NY, NZ), F32), pltpu.VMEM((LC, NY, NZ), BF16), pltpu.VMEM(vy.shape, BF16), pltpu.VMEM(vz.shape, BF16)],
+        out_specs=[VMEM] * 3,
+        out_shape=[pltpu.VMEM((LC, NY, NZ), F32), pltpu.VMEM(vy.shape, BF16), pltpu.VMEM(vz.shape, BF16)],
         scratch_shapes=[pltpu.VMEM((2, 2, rows, rows), BF16)],
         name="bypass",
         compiler_params=PARAMS,
@@ -266,10 +263,13 @@
 
 
 GELU = float(np.sqrt(2.0 / np.pi))
-TOGETHER = 2
-
-
-def inverse_kernel(h_ref, vy_ref, vz_ref, b_ref, f_ref, o_hbm, a_ref, out_ref, sems):
+TOGETHER = 1
+
+
+def inverse_kernel(h_ref, vy_ref, vz_ref, b_ref, f_hbm, o_hbm, a_ref, f_ref, out_ref, sems, f_sems):
+    loads = [pltpu.make_async_copy(f_hbm.at[o], f_ref.at[o], f_sems.at[o]) for o in range(LC)]
+    for load in loads:
+        load.start()
     sides = []
     for b in range(KB):
         sides.append(jnp.concatenate([h_ref[rows_of(b, n, part), :] for part in range(2) for n in range(PX)], 0).T)
@@ -286,6 +286,9 @@
         high, low = split(jnp.concatenate(parts, 0))
         half = dot(jnp.concatenate([high, low, high], 0).T, vz_ref[...]) + b_ref[o]
         bend = jnp.tanh(half * (2.0 * GELU + (8.0 * 0.044715 * GELU) * (half * half)))
+        if o in (0, LC // 4):
+            for load in loads[o : LC // 4 if o == 0 else LC]:
+                load.wait()
         out_ref[o] = (f_ref[o].astype(F32) + half) + half * bend
         if (o + 1) % TOGETHER == 0:
             rows = pl.ds(o + 1 - TOGETHER, TOGETHER)
@@ -298,17 +301,19 @@
 def inverse(sent, vy, vz, pre, field):
     return pl.pallas_call(
         inverse_kernel,
-        in_specs=[VMEM] * 5,
+        in_specs=[VMEM] * 4 + [pl.BlockSpec(memory_space=pl.ANY)],
         out_specs=pl.BlockSpec(memory_space=pl.ANY),
         out_shape=jax.ShapeDtypeStruct((LC, NY, NZ), F32),
         scratch_shapes=[
             pltpu.VMEM((KB * LC * K8, 2 * NY), F32),
+            pltpu.VMEM((LC, NY, NZ), BF16),
             pltpu.VMEM((LC, NY, NZ), F32),
             pltpu.SemaphoreType.DMA((LC // TOGETHER,)),
+            pltpu.SemaphoreType.DMA((LC,)),
         ],
         name="inverse",
         compiler_params=PARAMS,
-    )(*near(sent, vy, vz, pre, field))
+    )(*near(sent, vy, vz, pre), *far(field))
 
 
 def exchange(value):
@@ -325,13 +330,13 @@
     modes = exchange(forward(field, tz, wy))
 
     core = lax.axis_index("ch").astype(jnp.int32)[None]
-    pre, near_field, vy, vz = bypass_of(core, bypass_bias, bypass_weights[0].T, field, other, vy, vz)
+    pre, vy, vz = bypass_of(core, bypass_bias, bypass_weights[0].T, field, other, vy, vz)
 
     weights = spectral_weights[0].transpose(0, 1, 3, 4, 2).reshape(2, MX, LC * K8, C)
     weights, wx, vx = stage(weights, wx, vx)
     both = lax.all_gather(x_forward(modes, wx), "ch")
     back = exchange(mix(both, weights, vx))
-    return inverse(back, vy, vz, pre, near_field)[None]
+    return inverse(back, vy, vz, pre, field)[None]
 
 
 def solution(mesh):

time: 125 us -> 126 us (level)
  no operation moved by 1% of the time
where the time goes in v6:
time: 126 us
  starting transfers between devices  65.3 us (52%)
  waiting for transfers between devices  42.3 us (34%)
  Pallas kernels  14 us (11%)
  blocking collectives  1.88 us (1%)
  other arithmetic  1.31 us (1%)
    all_to_all x2, starting transfers between devices, exchange(): sent = lax.all_to_all(sent, ('pz', 'px'), 0, 0, tiled=True)  63.3 us
    all_to_all x2, waiting for transfers between devices, exchange(): sent = lax.all_to_all(sent, ('pz', 'px'), 0, 0, tiled=True)  42.3 us
    pallas_call x1, Pallas kernels, bypass_of(): pl.pallas_call(bypass_kernel, grid=(NY // BYPASS_ROWS,), in_specs=[smem,...  6.3 us
    pallas_call x1, Pallas kernels, inverse(): pl.pallas_call(inverse_kernel, in_specs=[VMEM] * 4 + [pl.BlockSpec(memory...  3.04 us
  transfers between devices with their start and end apart: 3, of which 2 were waited for; matrix products, arithmetic and copies ran while one was open for 1% of the time, Pallas kernels for 2%

profile of v6, /device:TPU:40, one launch (start us, length us, event | category | flops | bytes accessed | tf_op | source)
XLA Modules:
  0.0 125.9 jit_solution(1335201788351215805)
XLA Ops:
  0.0 0.0 copy-start
  0.0 2.4 %forward.1 = f32[256,128]{1,0:T(8,128)S(1)} custom-call(bf16[16,128,256]{2,1,0:T(8,128)(2,1)} %bitcast.19, bf16[128,256]{1,0:T(8,128)(2,1)} %constant.16.clone.tz_hbm, bf16[128,256]{1,0:T(8,128)(2,1)} %constant.17.clone.wy_hbm), custom_call_target="tpu_custom_call" | custom-call | tf_op jit(solution)/shard_map/forward/pallas_call | solution.py:127
  2.4 0.6 convert_element_type.16
  3.0 53.2 %all-to-all-start = ((f16[128,2,128]{2,1,0:T(2,128)(2,1)}), f16[128,2,128]{2,1,0:T(2,128)(2,1)S(1)}, u32[]{:S(2)}, u32[]{:S(2)}) async-start(f16[128,2,128]{2,1,0:T(2,128)(2,1)} %bitcast.1), calls=%async_computation | async-start | bytes 131072 | tf_op jit(solution)/shard_map/all_to_all | solution.py:321
  56.2 2.0 %collective-permute-start = (bf16[16,128,256]{2,1,0:T(8,128)(2,1)}, bf16[16,128,256]{2,1,0:T(8,128)(2,1)S(1)}, u32[]{:S(2)}, u32[]{:S(2)}) collective-permute-start(bf16[16,128,256]{2,1,0:T(8,128)(2,1)} %bitcast.20), channel_id=1, source_target_pairs={{0,1},{1,0},{2,3},{3,2},{4,5},{5,4},{6,7},{7,6},{8,9},{9,8},{10,11... | collective-permute-start | bytes 3145736 | tf_op jit(solution)/shard_map/ppermute | solution.py:328
  58.2 1.7 %stage.1 = (f32[2,32,16,128]{3,2,1,0:T(8,128)S(1)}, bf16[64,256]{1,0:T(8,128)(2,1)S(1)}, bf16[256,96]{1,0:T(8,128)(2,1)S(1)}) custom-call(bf16[2,16,128,32]{3,2,1,0:T(8,128)(2,1)} %bitcast.23, bf16[64,256]{1,0:T(8,128)(2,1)} %constant.20.clone.wx_in, bf16[256,96]{1,0:T(8,128)(2,1)} %constant.21.clone.vx_in), custom_call_target="tpu_custom_call" | custom-call | tf_op jit(solution)/shard_map/stage/pallas_call | solution.py:252
  59.9 19.1 %all-to-all-done = f16[128,2,128]{2,1,0:T(2,128)(2,1)S(1)} async-done(((f16[128,2,128]{2,1,0:T(2,128)(2,1)}), f16[128,2,128]{2,1,0:T(2,128)(2,1)S(1)}, u32[]{:S(2)}, u32[]{:S(2)}) %all-to-all-start) | async-done | bytes 65568 | tf_op jit(solution)/shard_map/all_to_all | solution.py:321
  79.1 0.1 x_forward.1
  79.2 1.9 %all-gather = f32[64,128]{1,0:T(8,128)S(1)} all-gather(f32[32,128]{1,0:T(8,128)S(1)} %x_forward.1), channel_id=2, replica_groups=mesh['grp'=2,'px'=4,'pz'=32,'ch'=2] {'ch'}, dimensions={0}, use_global_device_ids=true | all-gather | bytes 49152 | tf_op jit(solution)/shard_map/all_gather | solution.py:337
  81.1 0.4 mix.1
  81.5 0.7 convert_element_type.19
  82.2 10.1 %all-to-all-start.1 = ((f16[128,2,128]{2,1,0:T(2,128)(2,1)}), f16[128,2,128]{2,1,0:T(2,128)(2,1)S(1)}, u32[]{:S(2)}, u32[]{:S(2)}) async-start(f16[128,2,128]{2,1,0:T(2,128)(2,1)} %bitcast.7), calls=%async_computation.1 | async-start | bytes 131072 | tf_op jit(solution)/shard_map/all_to_all | solution.py:321
  92.3 23.2 %all-to-all-done.1 = f16[128,2,128]{2,1,0:T(2,128)(2,1)S(1)} async-done(((f16[128,2,128]{2,1,0:T(2,128)(2,1)}), f16[128,2,128]{2,1,0:T(2,128)(2,1)S(1)}, u32[]{:S(2)}, u32[]{:S(2)}) %all-to-all-start.1) | async-done | bytes 65568 | tf_op jit(solution)/shard_map/all_to_all | solution.py:321
  115.6 0.0 collective-permute-done.g_ref
  115.6 0.0 copy-start.1
  115.6 1.0 copy-done.1
  116.6 0.0 copy-done
  116.6 6.3 %bypass.1 = (f32[16,128,256]{2,1,0:T(8,128)S(1)}, bf16[2,64,256]{2,1,0:T(8,128)(2,1)S(1)}, bf16[192,256]{1,0:T(8,128)(2,1)S(1)}) custom-call(s32[1]{0:T(128)} %bitcast.9.core_ref, f32[1,16]{1,0:T(1,128)S(1)} %copy-done, f32[16,32]{1,0:T(8,128)} %bitcast.26, bf16[16,128,256]{2,1,0:T(8,128)(2,1)} %bitcast.21, bf16[16,128,256]{2,1,0:T(8,128)(2,1)} %copy-done.1, ...), custom_call_target="tpu_custom_call" | custom-call | tf_op jit(solution)/shard_map/bypass/pallas_call | solution.py:230
  122.9 3.0 %inverse.1 = f32[16,128,256]{2,1,0:T(8,128)} custom-call(f32[256,128]{1,0:T(8,128)S(1)} %convert.3.h_ref, bf16[2,64,256]{2,1,0:T(8,128)(2,1)S(1)} %get-tuple-element.14.vy_ref, bf16[192,256]{1,0:T(8,128)(2,1)S(1)} %get-tuple-element.15.vz_ref, f32[16,128,256]{2,1,0:T(8,128)S(1)} %get-tuple-element.16.b_ref, bf16[16,128,256]{2,1,0:T(8,128)(2,1)} %bitcast.22), custom_call_target="tpu_custom_call" | custom-call | tf_op jit(solution)/shard_map/inverse/pallas_call | solution.py:302
  (2 shorter events, 0.0 us)
Async XLA Ops:
  0.0 116.6 %copy-start = (f32[1,16]{1,0:T(1,128)S(1)}, f32[1,16]{1,0:T(1,128)}, u32[]{:S(2)}) copy-start(f32[1,16]{1,0:T(1,128)} %bias_ref.1) | copy-start | bytes 196
  3.0 76.0 %all-to-all-start = ((f16[128,2,128]{2,1,0:T(2,128)(2,1)}), f16[128,2,128]{2,1,0:T(2,128)(2,1)S(1)}, u32[]{:S(2)}, u32[]{:S(2)}) async-start(f16[128,2,128]{2,1,0:T(2,128)(2,1)} %bitcast.1), calls=%async_computation | async-start | bytes 131072 | tf_op jit(solution)/shard_map/all_to_all | solution.py:321
  56.2 59.4 %collective-permute-start = (bf16[16,128,256]{2,1,0:T(8,128)(2,1)}, bf16[16,128,256]{2,1,0:T(8,128)(2,1)S(1)}, u32[]{:S(2)}, u32[]{:S(2)}) collective-permute-start(bf16[16,128,256]{2,1,0:T(8,128)(2,1)} %bitcast.20), channel_id=1, source_target_pairs={{0,1},{1,0},{2,3},{3,2},{4,5},{5,4},{6,7},{7,6},{8,9},{9,8},{10,11... | collective-permute-start | bytes 3145736 | tf_op jit(solution)/shard_map/ppermute | solution.py:328
  82.2 33.4 %all-to-all-start.1 = ((f16[128,2,128]{2,1,0:T(2,128)(2,1)}), f16[128,2,128]{2,1,0:T(2,128)(2,1)S(1)}, u32[]{:S(2)}, u32[]{:S(2)}) async-start(f16[128,2,128]{2,1,0:T(2,128)(2,1)} %bitcast.7), calls=%async_computation.1 | async-start | bytes 131072 | tf_op jit(solution)/shard_map/all_to_all | solution.py:321
  115.6 1.0 copy-start.1

commit v7 on v5

--- a/solution.py
+++ b/solution.py
@@ -7,7 +7,7 @@
 from jax import lax
 from jax.experimental import pallas as pl
 from jax.experimental.pallas import tpu as pltpu
-from jax.sharding import Mesh, PartitionSpec as P
+from jax.sharding import PartitionSpec as P
 
 C = 32
 NX = 128
@@ -20,7 +20,9 @@
 K8 = 8
 LC = 16
 PX, PZ = 4, 32
-ORDER = [(place % PX) * PZ + place // PX for place in range(PX * PZ)]
+FIRST_Z = 28
+ORDER = [(place % PX) * PZ + (place // PX + FIRST_Z) % PZ for place in range(PX * PZ)]
+TURNED = [n * 8 + (m + FIRST_Z // KB) % 8 for n in range(PX) for m in range(8)]
 
 F32 = jnp.float32
 F16 = jnp.float16
@@ -46,7 +48,7 @@
 @functools.cache
 def constants():
     cos_x, sin_x = (table[:, ORDER] for table in tables(NX, MX))
-    cos_y, sin_y = tables(NY, MY)
+    cos_y, sin_y = (table[TURNED] for table in tables(NY, MY))
     cos_z, sin_z = tables(NZ, MZ)
     tz = np.concatenate(halves(np.concatenate([cos_z, -sin_z], 0) * NZ**-0.5), 0)
     wy = np.concatenate([np.concatenate([cos_y, sin_y], 1), np.concatenate([-sin_y, cos_y], 1)], 0)
@@ -313,7 +315,7 @@
 
 def exchange(value):
     sent = value.astype(F16).reshape(NX, 2, LC * K8)
-    sent = lax.all_to_all(sent, ("pz", "px"), 0, 0, tiled=True)
+    sent = lax.all_to_all(sent, "pen", 0, 0, axis_index_groups=[ORDER], tiled=True)
     return sent.reshape(2 * NX, LC * K8).astype(F32)
 
 
@@ -335,18 +337,15 @@
 
 
 def solution(mesh):
-    groups, _, cores = mesh.devices.shape
-    chips = Mesh(mesh.devices.reshape(groups, PX, PZ, cores), ("grp", "px", "pz", "ch"))
-
     return jax.shard_map(
         local,
-        mesh=chips,
+        mesh=mesh,
         in_specs=(
-            P(("grp", "px", "pz"), "ch", None, None),
-            P(None, None, None, None, "ch", ("px", "pz")),
+            P(("grp", "pen"), "ch", None, None),
+            P(None, None, None, None, "ch", "pen"),
             P(None, None, "ch"),
             P(None, "ch"),
         ),
-        out_specs=P(("grp", "px", "pz"), "ch", None, None),
+        out_specs=P(("grp", "pen"), "ch", None, None),
         check_vma=False,
     )

time: 125 us -> 124 us (level)
  waiting for transfers between devices: 42.3 us -> 38.6 us
  starting transfers between devices: 65.3 us -> 67.8 us
    all_to_all x2, waiting for transfers between devices: 42.3 us -> 38.6 us  [exchange(): lax.all_to_all(sent, 'pen', 0, 0, axis_index_groups=[ORDER], tiled=True)]
    all_to_all x2, starting transfers between devices: 63.3 us -> 65.9 us  [exchange(): lax.all_to_all(sent, 'pen', 0, 0, axis_index_groups=[ORDER], tiled=True)]
where the time goes in v7:
time: 124 us
  starting transfers between devices  67.8 us (55%)
  waiting for transfers between devices  38.6 us (31%)
  Pallas kernels  13.3 us (11%)
  blocking collectives  1.88 us (2%)
  other arithmetic  1.31 us (1%)
    all_to_all x2, starting transfers between devices, exchange(): lax.all_to_all(sent, 'pen', 0, 0, axis_index_groups=[ORDER], tiled=True)  65.9 us
    all_to_all x2, waiting for transfers between devices, exchange(): lax.all_to_all(sent, 'pen', 0, 0, axis_index_groups=[ORDER], tiled=True)  38.6 us
    pallas_call x1, Pallas kernels, bypass_of(): pl.pallas_call(bypass_kernel, grid=(NY // BYPASS_ROWS,), in_specs=[smem,...  6.31 us
  transfers between devices with their start and end apart: 3, of which 2 were waited for; matrix products, arithmetic and copies ran while one was open for 1% of the time, Pallas kernels for 2%

profile of v7, /device:TPU:40, one launch (start us, length us, event | category | flops | bytes accessed | tf_op | source)
XLA Modules:
  0.0 124.0 jit_solution(4411982559928397608)
XLA Ops:
  0.0 0.0 copy-start
  0.0 2.3 %forward.1 = f32[256,128]{1,0:T(8,128)S(1)} custom-call(bf16[16,128,256]{2,1,0:T(8,128)(2,1)} %bitcast.19, bf16[128,256]{1,0:T(8,128)(2,1)} %constant.16.clone.tz_hbm, bf16[128,256]{1,0:T(8,128)(2,1)} %constant.17.clone.wy_hbm), custom_call_target="tpu_custom_call" | custom-call | tf_op jit(solution)/shard_map/forward/pallas_call | solution.py:131
  2.3 0.6 convert_element_type.16
  2.9 53.9 %all-to-all-start = ((f16[128,2,128]{2,1,0:T(2,128)(2,1)}), f16[128,2,128]{2,1,0:T(2,128)(2,1)S(1)}, u32[]{:S(2)}, u32[]{:S(2)}) async-start(f16[128,2,128]{2,1,0:T(2,128)(2,1)} %bitcast.1), calls=%async_computation | async-start | bytes 131072 | tf_op jit(solution)/shard_map/all_to_all | solution.py:318
  56.8 2.0 %collective-permute-start = (bf16[16,128,256]{2,1,0:T(8,128)(2,1)}, bf16[16,128,256]{2,1,0:T(8,128)(2,1)S(1)}, u32[]{:S(2)}, u32[]{:S(2)}) collective-permute-start(bf16[16,128,256]{2,1,0:T(8,128)(2,1)} %bitcast.20), channel_id=1, source_target_pairs={{0,1},{1,0},{2,3},{3,2},{4,5},{5,4},{6,7},{7,6},{8,9},{9,8},{10,11... | collective-permute-start | bytes 3145736 | tf_op jit(solution)/shard_map/ppermute | solution.py:325
  58.8 1.7 %stage.1 = (f32[2,32,16,128]{3,2,1,0:T(8,128)S(1)}, bf16[64,256]{1,0:T(8,128)(2,1)S(1)}, bf16[256,96]{1,0:T(8,128)(2,1)S(1)}) custom-call(bf16[2,16,128,32]{3,2,1,0:T(8,128)(2,1)} %bitcast.22, bf16[64,256]{1,0:T(8,128)(2,1)} %constant.20.clone.wx_in, bf16[256,96]{1,0:T(8,128)(2,1)} %constant.21.clone.vx_in), custom_call_target="tpu_custom_call" | custom-call | tf_op jit(solution)/shard_map/stage/pallas_call | solution.py:257
  60.5 17.3 %all-to-all-done = f16[128,2,128]{2,1,0:T(2,128)(2,1)S(1)} async-done(((f16[128,2,128]{2,1,0:T(2,128)(2,1)}), f16[128,2,128]{2,1,0:T(2,128)(2,1)S(1)}, u32[]{:S(2)}, u32[]{:S(2)}) %all-to-all-start) | async-done | bytes 65568 | tf_op jit(solution)/shard_map/all_to_all | solution.py:318
  77.8 0.1 x_forward.1
  78.0 1.9 %all-gather = f32[64,128]{1,0:T(8,128)S(1)} all-gather(f32[32,128]{1,0:T(8,128)S(1)} %x_forward.1), channel_id=2, replica_groups=mesh['grp'=2,'pen'=128,'ch'=2] {'ch'}, dimensions={0}, use_global_device_ids=true | all-gather | bytes 49152 | tf_op jit(solution)/shard_map/all_gather | solution.py:334
  79.8 0.4 mix.1
  80.3 0.6 convert_element_type.19
  80.9 12.0 %all-to-all-start.1 = ((f16[128,2,128]{2,1,0:T(2,128)(2,1)}), f16[128,2,128]{2,1,0:T(2,128)(2,1)S(1)}, u32[]{:S(2)}, u32[]{:S(2)}) async-start(f16[128,2,128]{2,1,0:T(2,128)(2,1)} %bitcast.7), calls=%async_computation.1 | async-start | bytes 131072 | tf_op jit(solution)/shard_map/all_to_all | solution.py:318
  92.9 21.4 %all-to-all-done.1 = f16[128,2,128]{2,1,0:T(2,128)(2,1)S(1)} async-done(((f16[128,2,128]{2,1,0:T(2,128)(2,1)}), f16[128,2,128]{2,1,0:T(2,128)(2,1)S(1)}, u32[]{:S(2)}, u32[]{:S(2)}) %all-to-all-start.1) | async-done | bytes 65568 | tf_op jit(solution)/shard_map/all_to_all | solution.py:318
  114.3 0.0 collective-permute-done.g_ref
  114.3 0.0 copy-start.1
  114.3 1.0 copy-done.1
  115.3 0.0 copy-done
  115.3 6.3 %bypass.1 = (f32[16,128,256]{2,1,0:T(8,128)S(1)}, bf16[16,128,256]{2,1,0:T(8,128)(2,1)S(1)}, bf16[2,64,256]{2,1,0:T(8,128)(2,1)S(1)}, bf16[192,256]{1,0:T(8,128)(2,1)S(1)}) custom-call(s32[1]{0:T(128)} %bitcast.9.core_ref, f32[1,16]{1,0:T(1,128)S(1)} %copy-done, f32[16,32]{1,0:T(8,128)} %bitcast.25, bf16[16,128,256]{2,1,0:T(8,128)(2,1)} %bitcast.21, ...), custom_call_target="tpu_custom_call" | custom-call | tf_op jit(solution)/shard_map/bypass/pallas_call | solution.py:235
  121.6 2.3 %inverse.1 = f32[16,128,256]{2,1,0:T(8,128)} custom-call(f32[256,128]{1,0:T(8,128)S(1)} %convert.3.h_ref, bf16[2,64,256]{2,1,0:T(8,128)(2,1)S(1)} %get-tuple-element.15.vy_ref, bf16[192,256]{1,0:T(8,128)(2,1)S(1)} %get-tuple-element.16.vz_ref, f32[16,128,256]{2,1,0:T(8,128)S(1)} %get-tuple-element.17.b_ref, bf16[16,128,256]{2,1,0:T(8,128)(2,1)S(1)} %get-tuple-element.18.f_ref), custom_call_target="tpu_custom_call" | custom-call | tf_op jit(solution)/shard_map/inverse/pallas_call | solution.py:301
  (2 shorter events, 0.0 us)
Async XLA Ops:
  0.0 115.3 %copy-start = (f32[1,16]{1,0:T(1,128)S(1)}, f32[1,16]{1,0:T(1,128)}, u32[]{:S(2)}) copy-start(f32[1,16]{1,0:T(1,128)} %bias_ref.1) | copy-start | bytes 196
  2.9 74.8 %all-to-all-start = ((f16[128,2,128]{2,1,0:T(2,128)(2,1)}), f16[128,2,128]{2,1,0:T(2,128)(2,1)S(1)}, u32[]{:S(2)}, u32[]{:S(2)}) async-start(f16[128,2,128]{2,1,0:T(2,128)(2,1)} %bitcast.1), calls=%async_computation | async-start | bytes 131072 | tf_op jit(solution)/shard_map/all_to_all | solution.py:318
  56.8 57.5 %collective-permute-start = (bf16[16,128,256]{2,1,0:T(8,128)(2,1)}, bf16[16,128,256]{2,1,0:T(8,128)(2,1)S(1)}, u32[]{:S(2)}, u32[]{:S(2)}) collective-permute-start(bf16[16,128,256]{2,1,0:T(8,128)(2,1)} %bitcast.20), channel_id=1, source_target_pairs={{0,1},{1,0},{2,3},{3,2},{4,5},{5,4},{6,7},{7,6},{8,9},{9,8},{10,11... | collective-permute-start | bytes 3145736 | tf_op jit(solution)/shard_map/ppermute | solution.py:325
  80.9 33.4 %all-to-all-start.1 = ((f16[128,2,128]{2,1,0:T(2,128)(2,1)}), f16[128,2,128]{2,1,0:T(2,128)(2,1)S(1)}, u32[]{:S(2)}, u32[]{:S(2)}) async-start(f16[128,2,128]{2,1,0:T(2,128)(2,1)} %bitcast.7), calls=%async_computation.1 | async-start | bytes 131072 | tf_op jit(solution)/shard_map/all_to_all | solution.py:318
  114.3 1.0 copy-start.1

commit v8 on v7

--- a/solution.py
+++ b/solution.py
@@ -20,9 +20,10 @@
 K8 = 8
 LC = 16
 PX, PZ = 4, 32
-FIRST_Z = 28
-ORDER = [(place % PX) * PZ + (place // PX + FIRST_Z) % PZ for place in range(PX * PZ)]
-TURNED = [n * 8 + (m + FIRST_Z // KB) % 8 for n in range(PX) for m in range(8)]
+FIRST_Z = 24
+FIRST_X = 2
+ORDER = [(place + FIRST_X) % PX * PZ + (place // PX + FIRST_Z) % PZ for place in range(PX * PZ)]
+TURNED = [(n + FIRST_X) % PX * 8 + (m + FIRST_Z // KB) % 8 for n in range(PX) for m in range(8)]
 
 F32 = jnp.float32
 F16 = jnp.float16
@@ -82,7 +83,7 @@
     return lax.dot_general(a, b, (dims, ((), ())), preferred_element_type=F32)
 
 
-STEPS = 4
+STEPS = 2
 VMEM = pl.BlockSpec(memory_space=pltpu.VMEM)
 PARAMS = pltpu.CompilerParams(vmem_limit_bytes=16 << 20)
 

time: 124 us -> 123 us (level)
  waiting for transfers between devices: 38.6 us -> 24.4 us
  starting transfers between devices: 67.8 us -> 80.7 us
    all_to_all x2, waiting for transfers between devices: 38.6 us -> 24.4 us  [exchange(): lax.all_to_all(sent, 'pen', 0, 0, axis_index_groups=[ORDER], tiled=True)]
    all_to_all x2, starting transfers between devices: 65.9 us -> 78.8 us  [exchange(): lax.all_to_all(sent, 'pen', 0, 0, axis_index_groups=[ORDER], tiled=True)]
where the time goes in v8:
time: 123 us; the launch traced here: 122 us
  starting transfers between devices  80.7 us (66%)
  waiting for transfers between devices  24.4 us (20%)
  Pallas kernels  13.1 us (11%)
  blocking collectives  1.88 us (2%)
  other arithmetic  1.31 us (1%)
    all_to_all x2, starting transfers between devices, exchange(): lax.all_to_all(sent, 'pen', 0, 0, axis_index_groups=[ORDER], tiled=True)  78.8 us
    all_to_all x2, waiting for transfers between devices, exchange(): lax.all_to_all(sent, 'pen', 0, 0, axis_index_groups=[ORDER], tiled=True)  24.4 us
    pallas_call x1, Pallas kernels, bypass_of(): pl.pallas_call(bypass_kernel, grid=(NY // BYPASS_ROWS,), in_specs=[smem,...  6.31 us
  transfers between devices with their start and end apart: 3, of which 2 were waited for; matrix products, arithmetic and copies ran while one was open for 1% of the time, Pallas kernels for 2%

profile of v8, /device:TPU:40, one launch (start us, length us, event | category | flops | bytes accessed | tf_op | source)
XLA Modules:
  0.0 122.4 jit_solution(15104534127526393303)
XLA Ops:
  0.0 0.0 copy-start
  0.0 2.1 %forward.1 = f32[256,128]{1,0:T(8,128)S(1)} custom-call(bf16[16,128,256]{2,1,0:T(8,128)(2,1)} %bitcast.19, bf16[128,256]{1,0:T(8,128)(2,1)} %constant.16.clone.tz_hbm, bf16[128,256]{1,0:T(8,128)(2,1)} %constant.17.clone.wy_hbm), custom_call_target="tpu_custom_call" | custom-call | tf_op jit(solution)/shard_map/forward/pallas_call | solution.py:132
  2.1 0.6 convert_element_type.16
  2.7 59.7 %all-to-all-start = ((f16[128,2,128]{2,1,0:T(2,128)(2,1)}), f16[128,2,128]{2,1,0:T(2,128)(2,1)S(1)}, u32[]{:S(2)}, u32[]{:S(2)}) async-start(f16[128,2,128]{2,1,0:T(2,128)(2,1)} %bitcast.1), calls=%async_computation | async-start | bytes 131072 | tf_op jit(solution)/shard_map/all_to_all | solution.py:319
  62.5 2.0 %collective-permute-start = (bf16[16,128,256]{2,1,0:T(8,128)(2,1)}, bf16[16,128,256]{2,1,0:T(8,128)(2,1)S(1)}, u32[]{:S(2)}, u32[]{:S(2)}) collective-permute-start(bf16[16,128,256]{2,1,0:T(8,128)(2,1)} %bitcast.20), channel_id=1, source_target_pairs={{0,1},{1,0},{2,3},{3,2},{4,5},{5,4},{6,7},{7,6},{8,9},{9,8},{10,11... | collective-permute-start | bytes 3145736 | tf_op jit(solution)/shard_map/ppermute | solution.py:326
  64.5 1.7 %stage.1 = (f32[2,32,16,128]{3,2,1,0:T(8,128)S(1)}, bf16[64,256]{1,0:T(8,128)(2,1)S(1)}, bf16[256,96]{1,0:T(8,128)(2,1)S(1)}) custom-call(bf16[2,16,128,32]{3,2,1,0:T(8,128)(2,1)} %bitcast.22, bf16[64,256]{1,0:T(8,128)(2,1)} %constant.20.clone.wx_in, bf16[256,96]{1,0:T(8,128)(2,1)} %constant.21.clone.vx_in), custom_call_target="tpu_custom_call" | custom-call | tf_op jit(solution)/shard_map/stage/pallas_call | solution.py:258
  66.2 10.2 %all-to-all-done = f16[128,2,128]{2,1,0:T(2,128)(2,1)S(1)} async-done(((f16[128,2,128]{2,1,0:T(2,128)(2,1)}), f16[128,2,128]{2,1,0:T(2,128)(2,1)S(1)}, u32[]{:S(2)}, u32[]{:S(2)}) %all-to-all-start) | async-done | bytes 65568 | tf_op jit(solution)/shard_map/all_to_all | solution.py:319
  76.4 0.1 x_forward.1
  76.6 1.9 %all-gather = f32[64,128]{1,0:T(8,128)S(1)} all-gather(f32[32,128]{1,0:T(8,128)S(1)} %x_forward.1), channel_id=2, replica_groups=mesh['grp'=2,'pen'=128,'ch'=2] {'ch'}, dimensions={0}, use_global_device_ids=true | all-gather | bytes 49152 | tf_op jit(solution)/shard_map/all_gather | solution.py:335
  78.4 0.4 mix.1
  78.9 0.7 convert_element_type.19
  79.5 19.0 %all-to-all-start.1 = ((f16[128,2,128]{2,1,0:T(2,128)(2,1)}), f16[128,2,128]{2,1,0:T(2,128)(2,1)S(1)}, u32[]{:S(2)}, u32[]{:S(2)}) async-start(f16[128,2,128]{2,1,0:T(2,128)(2,1)} %bitcast.7), calls=%async_computation.1 | async-start | bytes 131072 | tf_op jit(solution)/shard_map/all_to_all | solution.py:319
  98.6 14.2 %all-to-all-done.1 = f16[128,2,128]{2,1,0:T(2,128)(2,1)S(1)} async-done(((f16[128,2,128]{2,1,0:T(2,128)(2,1)}), f16[128,2,128]{2,1,0:T(2,128)(2,1)S(1)}, u32[]{:S(2)}, u32[]{:S(2)}) %all-to-all-start.1) | async-done | bytes 65568 | tf_op jit(solution)/shard_map/all_to_all | solution.py:319
  112.7 0.0 collective-permute-done.g_ref
  112.8 0.0 copy-start.1
  112.8 1.0 copy-done.1
  113.7 0.0 copy-done
  113.7 6.3 %bypass.1 = (f32[16,128,256]{2,1,0:T(8,128)S(1)}, bf16[16,128,256]{2,1,0:T(8,128)(2,1)S(1)}, bf16[2,64,256]{2,1,0:T(8,128)(2,1)S(1)}, bf16[192,256]{1,0:T(8,128)(2,1)S(1)}) custom-call(s32[1]{0:T(128)} %bitcast.9.core_ref, f32[1,16]{1,0:T(1,128)S(1)} %copy-done, f32[16,32]{1,0:T(8,128)} %bitcast.25, bf16[16,128,256]{2,1,0:T(8,128)(2,1)} %bitcast.21, ...), custom_call_target="tpu_custom_call" | custom-call | tf_op jit(solution)/shard_map/bypass/pallas_call | solution.py:236
  120.1 2.3 %inverse.1 = f32[16,128,256]{2,1,0:T(8,128)} custom-call(f32[256,128]{1,0:T(8,128)S(1)} %convert.3.h_ref, bf16[2,64,256]{2,1,0:T(8,128)(2,1)S(1)} %get-tuple-element.15.vy_ref, bf16[192,256]{1,0:T(8,128)(2,1)S(1)} %get-tuple-element.16.vz_ref, f32[16,128,256]{2,1,0:T(8,128)S(1)} %get-tuple-element.17.b_ref, bf16[16,128,256]{2,1,0:T(8,128)(2,1)S(1)} %get-tuple-element.18.f_ref), custom_call_target="tpu_custom_call" | custom-call | tf_op jit(solution)/shard_map/inverse/pallas_call | solution.py:302
  (2 shorter events, 0.0 us)
Async XLA Ops:
  0.0 113.7 %copy-start = (f32[1,16]{1,0:T(1,128)S(1)}, f32[1,16]{1,0:T(1,128)}, u32[]{:S(2)}) copy-start(f32[1,16]{1,0:T(1,128)} %bias_ref.1) | copy-start | bytes 196
  2.7 73.7 %all-to-all-start = ((f16[128,2,128]{2,1,0:T(2,128)(2,1)}), f16[128,2,128]{2,1,0:T(2,128)(2,1)S(1)}, u32[]{:S(2)}, u32[]{:S(2)}) async-start(f16[128,2,128]{2,1,0:T(2,128)(2,1)} %bitcast.1), calls=%async_computation | async-start | bytes 131072 | tf_op jit(solution)/shard_map/all_to_all | solution.py:319
  62.5 50.3 %collective-permute-start = (bf16[16,128,256]{2,1,0:T(8,128)(2,1)}, bf16[16,128,256]{2,1,0:T(8,128)(2,1)S(1)}, u32[]{:S(2)}, u32[]{:S(2)}) collective-permute-start(bf16[16,128,256]{2,1,0:T(8,128)(2,1)} %bitcast.20), channel_id=1, source_target_pairs={{0,1},{1,0},{2,3},{3,2},{4,5},{5,4},{6,7},{7,6},{8,9},{9,8},{10,11... | collective-permute-start | bytes 3145736 | tf_op jit(solution)/shard_map/ppermute | solution.py:326
  79.5 33.2 %all-to-all-start.1 = ((f16[128,2,128]{2,1,0:T(2,128)(2,1)}), f16[128,2,128]{2,1,0:T(2,128)(2,1)S(1)}, u32[]{:S(2)}, u32[]{:S(2)}) async-start(f16[128,2,128]{2,1,0:T(2,128)(2,1)} %bitcast.7), calls=%async_computation.1 | async-start | bytes 131072 | tf_op jit(solution)/shard_map/all_to_all | solution.py:319
  112.8 1.0 copy-start.1
